TPU v7x, 32 devices: a whole 2x2x4 slice. The times are simulated.
32 devices in a mesh: dp: 4 (over y, core), tensor: 8 (over z, x).
Axes of the slice: x: 2, y: 2, z: 4, core: 2. Of those that a mesh axis runs over, the one named last changes fastest.
Arguments:
- tokens: bfloat16 [512, 1024], P('dp', 'tensor'), may hold values from -6 to 6
- init_noise: float32 [512, 1024], P('dp', 'tensor'), may hold values from -1 to 1
- segment_ids: int32 [512], P('dp'), may hold values from 0 to 7, never falling along the last dimension, each value on 1 to 256 neighbouring positions
- target: float32 [512, 1024], P('dp', 'tensor'), may hold values from -6 to 6
- norm_gain: float32 [1024], replicated, may hold values from 0.1 to 1.9
- weight_in: bfloat16 [1024, 32768], P(None, 'tensor'), may hold values from -0.1875 to 0.1875
- weight_out: bfloat16 [32768, 1024], P('tensor'), may hold values from -0.03125 to 0.03125
- moment_in: float32 [1024, 32768], P('dp', 'tensor'), may hold values from -1.5 to 1.5
- moment_out: float32 [32768, 1024], P('tensor', 'dp'), may hold values from -1.5 to 1.5
Outputs:
- new_weight_in: bfloat16 [1024, 32768], P('dp', 'tensor')
- new_weight_out: bfloat16 [32768, 1024], P('tensor', 'dp')
- new_moment_in: float32 [1024, 32768], P('dp', 'tensor')
- new_moment_out: float32 [32768, 1024], P('tensor', 'dp')
- perturbation: float32 [512, 1024], P('dp', 'tensor')
Inputs may be any that keep to these rules, and one draw needn't show every extreme that they name: `segment_ids`: example ids never fall along the tokens; every example holds 1 to 256 tokens.
All inputs are finite; a program needn't handle non-finite values.
Results may differ from a plain program's by a relative error of at most 0.0051.
Values may be sent and summed in bfloat16 or wider, within the bound.
A program may use at most 128 MiB of HBM per device.

v0:
```python
import functools

import jax
import jax.numpy as jnp
from jax import lax
from jax.experimental import pallas as pl
from jax.experimental.pallas import tpu as pltpu
from jax.sharding import PartitionSpec as P

ASCENTS = 2

coeff = 0.7978845608
adv_init = 0.5
adv_step = 0.5
decay = 0.9
learn_rate = 0.01


def gelu_both(values):
    square = values * values
    tangent = jnp.tanh(coeff * (values + 0.044715 * square * values))
    half = 0.5 * (1.0 + tangent)
    slope = half + 0.5 * values * (1.0 - tangent * tangent) * coeff * (1.0 + 3.0 * 0.044715 * square)
    return values * half, slope


class Place:
    def __init__(self):
        self.dp_count, self.tensor_count = lax.axis_size("dp"), lax.axis_size("tensor")
        self.ys, self.zs = self.dp_count // 2, self.tensor_count // 2
        self.dp, self.tensor = lax.axis_index("dp"), lax.axis_index("tensor")
        self.y, self.core = self.dp // 2, self.dp % 2
        self.z, self.x = self.tensor // 2, self.tensor % 2


def enter(at):
    barrier = pltpu.get_barrier_semaphore()
    for step in range(1, at.tensor_count):
        there = (at.dp, lax.rem(at.tensor + step, at.tensor_count))
        pl.semaphore_signal(barrier, inc=1, device_id=there, device_id_type=pl.DeviceIdType.MESH)
    for step in range(1, at.dp_count):
        there = (lax.rem(at.dp + step, at.dp_count), at.tensor)
        pl.semaphore_signal(barrier, inc=1, device_id=there, device_id_type=pl.DeviceIdType.MESH)
    pl.semaphore_wait(barrier, at.tensor_count + at.dp_count - 2)


def send(source, target, sems, number, there):
    copy = pltpu.make_async_remote_copy(
        src_ref=source,
        dst_ref=target,
        send_sem=sems[0].at[number],
        recv_sem=sems[1].at[number],
        device_id=there,
        device_id_type=pl.DeviceIdType.MESH,
    )
    copy.start()
    return copy


def gather_copies(dp_count, tensor_count):
    zs, ys = tensor_count // 2, dp_count // 2
    return (zs - 1) + zs + 2 * zs * (ys - 1) + 2 * zs * ys


def gather(at, own_ref, whole_ref, sems):
    rows, cols = own_ref.shape
    numbers = iter(range(gather_copies(at.dp_count, at.tensor_count)))
    started, to_core = [], []

    def place(dp, tensor):
        span = pl.ds(pl.multiple_of(dp * rows, rows), rows)
        if len(whole_ref.shape) == 3:
            return (tensor, span)
        return (span, pl.ds(pl.multiple_of(tensor * cols, cols), cols))

    def block(dp, tensor):
        return whole_ref.at[place(dp, tensor)]

    def start(source, dp, tensor, there):
        copy = send(source, block(dp, tensor), sems, next(numbers), there)
        started.append(copy)
        return copy

    def share(source, dp, tensor):
        to_core.append(start(source, dp, tensor, (at.y * 2 + 1 - at.core, at.tensor)))

    other_x = (at.dp, at.z * 2 + 1 - at.x)
    along_z = {
        k: start(
            own_ref, at.dp, at.tensor, (at.dp, lax.rem(at.z + at.zs - k, at.zs) * 2 + at.x)
        )
        for k in range(1, at.zs)
    }
    whole_ref[place(at.dp, at.tensor)] = own_ref[...]
    along_x, along_y, corner = {}, {}, {}
    column = [lax.rem(at.z + k, at.zs) * 2 for k in range(at.zs)]
    line = [lax.rem(at.y + j, at.ys) * 2 + at.core for j in range(at.ys)]
    back = [lax.rem(at.y + at.ys - j, at.ys) * 2 + at.core for j in range(at.ys)]
    for k in range(at.zs):
        mine = column[k] + at.x
        source = own_ref
        if k:
            along_z[k].wait_recv()
            source = block(at.dp, mine)
        along_x[k] = start(source, at.dp, mine, other_x)
        for j in range(1, at.ys):
            along_y[k, j] = start(source, at.dp, mine, (back[j], at.tensor))
        share(source, at.dp, mine)
    for k in range(at.zs):
        mine, beside = column[k] + at.x, column[k] + 1 - at.x
        along_x[k].wait_recv()
        for j in range(1, at.ys):
            if k % 2 == 0:
                corner[k, j] = start(
                    block(at.dp, beside), at.dp, beside, (back[j], at.tensor)
                )
        share(block(at.dp, beside), at.dp, beside)
        for j in range(1, at.ys):
            along_y[k, j].wait_recv()
            if k % 2 == 1:
                corner[k, j] = start(block(line[j], mine), line[j], mine, other_x)
            share(block(line[j], mine), line[j], mine)
    for k in range(at.zs):
        beside = column[k] + 1 - at.x
        for j in range(1, at.ys):
            corner[k, j].wait_recv()
            share(block(line[j], beside), line[j], beside)
    for copy in to_core:
        copy.wait_recv()
    for copy in started:
        copy.wait_send()


def scatter_sum(at, partial_ref, landing, sems):
    cols = landing.shape[2]

    def own(tensor):
        if len(partial_ref.shape) == 3:
            return (tensor,)
        return (slice(None), pl.ds(pl.multiple_of(tensor * cols, cols), cols))

    copies = []
    for step in range(1, at.tensor_count):
        there = lax.rem(at.tensor + step, at.tensor_count)
        copies.append(
            send(
                partial_ref.at[own(there)], landing.at[step - 1], sems, step - 1, (at.dp, there)
            )
        )
    value = partial_ref[own(at.tensor)].astype(jnp.float32)
    for step, copy in enumerate(copies):
        copy.wait_recv()
        value = value + landing[step].astype(jnp.float32)
    for copy in copies:
        copy.wait_send()
    return value


def first_kernel(emb_ref, whole_ref, *sems):
    at = Place()
    enter(at)
    gather(at, emb_ref, whole_ref, sems)


def forward_kernel(
    partial_ref, tokens_ref, perturb_ref, target_ref, whole_ref, out_grad_ref,
    landing, own, send_sum, recv_sum, send_all, recv_all, *, scale,
):
    at = Place()
    enter(at)
    mixed = scatter_sum(at, partial_ref, landing, (send_sum, recv_sum))
    embedded = tokens_ref[...].astype(jnp.float32) + perturb_ref[...]
    out_grad = (embedded + mixed - target_ref[...]) * scale
    own[...] = out_grad.astype(jnp.bfloat16)
    out_grad_ref[...] = out_grad
    gather(at, own, whole_ref, (send_all, recv_all))


def ascent_kernel(
    partial_ref, tokens_ref, perturb_ref, out_grad_ref, inv_ref, gain_ref, ids_ref,
    whole_ref, new_ref,
    landing, own, stats, stats_in, squares, squares_in,
    send_sum, recv_sum, send_stat, recv_stat, send_square, recv_square, send_all, recv_all,
    *, features,
):
    at = Place()
    enter(at)
    rows = own.shape[0]
    examples = squares.shape[0] // 2
    scaled = gain_ref[...] * scatter_sum(at, partial_ref, landing, (send_sum, recv_sum))
    tokens = tokens_ref[...].astype(jnp.float32)
    perturb = perturb_ref[...]
    emb = (tokens + perturb).astype(jnp.bfloat16).astype(jnp.float32)
    inv = inv_ref[...]
    base = out_grad_ref[...] + inv * scaled
    radial = emb * (inv * inv * inv * (1.0 / features))
    lane = lax.broadcasted_iota(jnp.int32, (rows, rows), 1)
    table = jnp.where(lane == 0, jnp.sum(scaled * emb, axis=1, keepdims=True), 0.0)
    table = jnp.where(lane == 1, jnp.sum(base * base, axis=1, keepdims=True), table)
    table = jnp.where(lane == 2, jnp.sum(base * radial, axis=1, keepdims=True), table)
    table = jnp.where(lane == 3, jnp.sum(radial * radial, axis=1, keepdims=True), table)
    own_stats = table.T[:8, :]
    stats[...] = own_stats
    copies = [
        send(
            stats, stats_in.at[step - 1], (send_stat, recv_stat), step - 1,
            (at.dp, lax.rem(at.tensor + step, at.tensor_count)),
        )
        for step in range(1, at.tensor_count)
    ]
    summed = own_stats
    for step, copy in enumerate(copies):
        copy.wait_recv()
        summed = summed + stats_in[step]
    for copy in copies:
        copy.wait_send()
    row_dot = summed[0:1, :]
    row_squares = (
        summed[1:2, :] - 2.0 * row_dot * summed[2:3, :] + row_dot * row_dot * summed[3:4, :]
    )
    label = lax.broadcasted_iota(jnp.int32, (examples, rows), 0)
    onehot = (label == ids_ref[...]).astype(jnp.float32)
    local = jnp.concatenate(
        [
            jnp.broadcast_to(
                jnp.sum(onehot * row_squares, axis=1, keepdims=True), (examples, rows)
            ),
            jnp.broadcast_to(jnp.sum(onehot, axis=1, keepdims=True), (examples, rows)),
        ],
        axis=0,
    )
    squares[...] = local
    copies = [
        send(
            squares, squares_in.at[step - 1], (send_square, recv_square), step - 1,
            (lax.rem(at.dp + step, at.dp_count), at.tensor),
        )
        for step in range(1, at.dp_count)
    ]
    for step, copy in enumerate(copies):
        copy.wait_recv()
        local = local + squares_in[step]
    for copy in copies:
        copy.wait_send()
    square_sums, counts = jnp.maximum(local[:examples], 0.0), local[examples:]
    root_mean = jnp.sqrt(square_sums / (jnp.maximum(counts, 1.0) * features) + 1e-06)
    token_scale = jnp.sum(onehot * (adv_step / root_mean), axis=0, keepdims=True)
    high = lax.broadcasted_iota(jnp.int32, (rows, rows), 0)
    columns = jnp.where(high == 0, token_scale, jnp.where(high == 1, row_dot, 0.0)).T
    perturb = perturb + (base - radial * columns[:, 1:2]) * columns[:, 0:1]
    new_ref[...] = perturb
    own[...] = (tokens + perturb).astype(jnp.bfloat16)
    gather(at, own, whole_ref, (send_all, recv_all))


def talk(kernel, number, out_shape, scratch, *args):
    vmem = pl.BlockSpec(memory_space=pltpu.VMEM)
    return pl.pallas_call(
        kernel,
        name=f"talk{number}",
        out_shape=out_shape,
        in_specs=[vmem] * len(args),
        out_specs=jax.tree.map(lambda _: vmem, out_shape),
        scratch_shapes=scratch,
        compiler_params=pltpu.CompilerParams(collective_id=number, has_side_effects=True),
    )(*args)


def shards(
    tokens, init_noise, segment_ids, target, norm_gain, weight_in, weight_out, moment_in, moment_out
):
    dp_count, tensor_count = lax.axis_size("dp"), lax.axis_size("tensor")
    rows, width = tokens.shape
    features = weight_in.shape[0]
    loss_scale = (rows * dp_count) ** (-0.5)
    me = lax.axis_index("dp")
    own_rows = moment_in.shape[0]
    examples = 2 * dp_count
    gain_own = lax.dynamic_slice_in_dim(norm_gain, lax.axis_index("tensor") * width, width, 0)
    dma = pltpu.SemaphoreType.DMA
    copies = gather_copies(dp_count, tensor_count)
    gather_sems = [dma((copies,)), dma((copies,))]
    sum_sems = [dma((tensor_count - 1,)), dma((tensor_count - 1,))]
    square_sems = [dma((dp_count - 1,)), dma((dp_count - 1,))]
    landing = pltpu.VMEM((tensor_count - 1, rows, width), jnp.bfloat16)
    own_block = pltpu.VMEM((rows, width), jnp.bfloat16)
    narrow = width % 128 != 0
    total = rows * dp_count
    whole = jax.ShapeDtypeStruct(
        (tensor_count, total, width) if narrow else (total, features), jnp.bfloat16
    )

    def flat(array):
        return array.transpose(1, 0, 2).reshape(total, features) if narrow else array

    def split(array):
        return array.reshape(rows, tensor_count, width).transpose(1, 0, 2) if narrow else array

    block = jax.ShapeDtypeStruct((rows, width), jnp.float32)
    perturb = adv_init * init_noise
    emb_bf = (tokens.astype(jnp.float32) + perturb).astype(jnp.bfloat16)
    gathered_bf = talk(first_kernel, 0, whole, gather_sems, emb_bf)
    grad_in = jnp.zeros(moment_in.shape, jnp.float32)
    grad_out = jnp.zeros(moment_out.shape, jnp.float32)
    for ascent in range(ASCENTS):
        gathered = flat(gathered_bf).astype(jnp.float32)
        inv_rms = lax.rsqrt(jnp.mean(gathered * gathered, axis=1, keepdims=True) + 1e-06)
        normed = (gathered * inv_rms * norm_gain).astype(jnp.bfloat16)
        preact = jnp.dot(normed, weight_in, preferred_element_type=jnp.float32)
        hidden, slope = gelu_both(preact)
        hidden = hidden.astype(jnp.bfloat16)
        hidden_own = lax.dynamic_slice_in_dim(hidden, me * rows, rows, 0)
        partial_value = jnp.dot(
            hidden_own, weight_out, preferred_element_type=jnp.float32
        ).astype(jnp.bfloat16)
        grad_whole, out_grad = talk(
            functools.partial(forward_kernel, scale=loss_scale), 1 + 2 * ascent, (whole, block),
            [landing, own_block, *sum_sems, *gather_sems],
            split(partial_value), tokens, perturb, target,
        )
        grad_whole = flat(grad_whole)
        hidden_grad = (
            jnp.dot(grad_whole, weight_out.T, preferred_element_type=jnp.float32) * slope
        ).astype(jnp.bfloat16)
        if ascent + 1 < ASCENTS:
            hidden_grad_own = lax.dynamic_slice_in_dim(hidden_grad, me * rows, rows, 0)
            normed_partial = jnp.dot(
                hidden_grad_own, weight_in.T, preferred_element_type=jnp.float32
            ).astype(jnp.bfloat16)
            inv_own = lax.dynamic_slice_in_dim(inv_rms, me * rows, rows, 0)
            small = pltpu.VMEM((8, rows), jnp.float32)
            gathered_bf, perturb = talk(
                functools.partial(ascent_kernel, features=features), 2 + 2 * ascent,
                (whole, block),
                [
                    landing, own_block, small,
                    pltpu.VMEM((tensor_count - 1, 8, rows), jnp.float32),
                    pltpu.VMEM((2 * examples, rows), jnp.float32),
                    pltpu.VMEM((dp_count - 1, 2 * examples, rows), jnp.float32),
                    *sum_sems, *sum_sems, *square_sems, *gather_sems,
                ],
                split(normed_partial), tokens, perturb, out_grad, inv_own,
                gain_own.reshape(1, width), segment_ids.reshape(1, rows),
            )
        normed_cols = lax.dynamic_slice_in_dim(normed, me * own_rows, own_rows, 1)
        grad_cols = lax.dynamic_slice_in_dim(grad_whole, me * own_rows, own_rows, 1)
        grad_in = grad_in + jnp.dot(normed_cols.T, hidden_grad, preferred_element_type=jnp.float32)
        grad_out = grad_out + jnp.dot(hidden.T, grad_cols, preferred_element_type=jnp.float32)
    own_in = lax.dynamic_slice_in_dim(weight_in, me * own_rows, own_rows, 0)
    own_out = lax.dynamic_slice_in_dim(weight_out, me * own_rows, own_rows, 1)
    new_moment_in = decay * moment_in + grad_in / ASCENTS
    new_moment_out = decay * moment_out + grad_out / ASCENTS
    new_weight_in = (own_in.astype(jnp.float32) - learn_rate * new_moment_in).astype(jnp.bfloat16)
    new_weight_out = (own_out.astype(jnp.float32) - learn_rate * new_moment_out).astype(
        jnp.bfloat16
    )
    return (new_weight_in, new_weight_out, new_moment_in, new_moment_out, perturb)


def solution(mesh):
    placed = (
        P("dp", "tensor"),
        P("dp", "tensor"),
        P("dp"),
        P("dp", "tensor"),
        P(),
        P(None, "tensor"),
        P("tensor", None),
        P("dp", "tensor"),
        P("tensor", "dp"),
    )
    return jax.shard_map(
        shards,
        mesh=mesh,
        in_specs=placed,
        out_specs=(
            P("dp", "tensor"),
            P("tensor", "dp"),
            P("dp", "tensor"),
            P("tensor", "dp"),
            P("dp", "tensor"),
        ),
        check_vma=False,
    )
```

profile of v0, /device:TPU:0, one launch (start us, length us, event | category | flops | bytes accessed | tf_op | source)
XLA Modules:
  0.0 203.9 jit_solution(7017409760090788228)
XLA Ops:
  0.6 1.3 dynamic-slice_bitcast_fusion.gain_ref
  1.9 1.5 broadcast_multiply_fusion
  3.4 19.3 %talk0.1 = bf16[512,1024]{1,0:T(8,128)(2,1)} custom-call(bf16[128,128]{1,0:T(8,128)(2,1)} %get-tuple-element.16.emb_ref), custom_call_target="tpu_custom_call" | custom-call | tf_op jit(solution)/shard_map/talk0/pallas_call | solution.py:258
  22.7 1.5 fusion.8
  24.2 1.5 fusion.10
  25.9 0.7 copy.14.inv_ref
  26.6 11.6 %multiply_convert_fusion.3 = (bf16[512,4096]{1,0:T(8,128)(2,1)S(1)}, f32[512,4096]{1,0:T(8,128)}) fusion(bf16[512,1024]{1,0:T(8,128)(2,1)S(1)} %fusion.10, bf16[1024,4096]{1,0:T(8,128)(2,1)} %param.14), kind=kOutput, calls=%fused_computation.10 | convolution fusion | flops 4313841664 | bytes 22020096 | tf_op jit(solution)/shard_map/dot_general | solution.py:309
  38.3 2.0 copy-done.1
  40.3 5.4 %convolution_convert_fusion.2.partial_ref = bf16[128,1024]{1,0:T(8,128)(2,1)} fusion(bf16[4096,1024]{1,0:T(8,128)(2,1)} %param.15, bf16[512,4096]{1,0:T(8,128)(2,1)S(1)} %get-tuple-element.17, s32[]{:T(128)S(6)} %select_n.7), kind=kOutput, calls=%fused_computation.32 | convolution fusion | flops 1073872896 | bytes 9699332 | tf_op jit(solution)/shard_map/dot_general | solution.py:313
  45.6 25.7 %talk1.1 = (bf16[512,1024]{1,0:T(8,128)(2,1)}, f32[128,128]{1,0:T(8,128)}) custom-call(bf16[128,1024]{1,0:T(8,128)(2,1)} %convolution_convert_fusion.2.partial_ref, bf16[128,128]{1,0:T(8,128)(2,1)} %tokens_ref.5, f32[128,128]{1,0:T(8,128)} %get-tuple-element.15.perturb_ref, f32[128,128]{1,0:T(8,128)} %target_ref.3), custom_call_target="tpu_custom_call" | custom-call | tf_op jit(solution)/shard_map/talk1/pallas_call | solution.py:258
  71.3 12.3 %multiply_convert_fusion.2 = bf16[512,4096]{1,0:T(8,128)(2,1)S(1)} fusion(f32[512,4096]{1,0:T(8,128)} %get-tuple-element.18, bf16[512,1024]{1,0:T(8,128)(2,1)} %get-tuple-element.10, bf16[4096,1024]{1,0:T(8,128)(2,1)} %param.15), kind=kOutput, calls=%fused_computation.9 | convolution fusion | flops 4332716032 | bytes 22020096 | tf_op jit(solution)/shard_map/dot_general | solution.py:323
  83.6 4.2 %fusion.18 = f32[4096,256]{1,0:T(8,128)} fusion(bf16[512,4096]{1,0:T(8,128)(2,1)S(1)} %copy-done.2, bf16[512,1024]{1,0:T(8,128)(2,1)} %get-tuple-element.10, s32[]{:T(128)S(6)} %select_n.6), kind=kOutput, calls=%fused_computation.37 | convolution fusion | flops 1073741824 | bytes 8650756 | tf_op jit(solution)/shard_map/dot_general | solution.py:348
  87.8 7.0 %convolution_convert_fusion.1.partial_ref = bf16[128,1024]{1,0:T(8,128)(2,1)} fusion(bf16[1024,4096]{1,0:T(8,128)(2,1)} %param.14, bf16[512,4096]{1,0:T(8,128)(2,1)S(1)} %multiply_convert_fusion.2, s32[]{:T(128)S(6)} %select_n.7), kind=kOutput, calls=%fused_computation.31 | convolution fusion | flops 1073872896 | bytes 9699332 | tf_op jit(solution)/shard_map/dot_general | solution.py:327
  94.8 3.4 %fusion.21 = f32[256,4096]{1,0:T(8,128)} fusion(bf16[512,4096]{1,0:T(8,128)(2,1)S(1)} %multiply_convert_fusion.2, bf16[512,1024]{1,0:T(8,128)(2,1)S(1)} %fusion.10, s32[]{:T(128)S(6)} %select_n.6), kind=kOutput, calls=%fused_computation.40 | convolution fusion | flops 1073741824 | bytes 8650756 | tf_op jit(solution)/shard_map/dot_general | solution.py:347
  98.2 31.7 %talk2.1 = (bf16[512,1024]{1,0:T(8,128)(2,1)}, f32[128,128]{1,0:T(8,128)}) custom-call(bf16[128,1024]{1,0:T(8,128)(2,1)} %convolution_convert_fusion.1.partial_ref, bf16[128,128]{1,0:T(8,128)(2,1)} %tokens_ref.5, f32[128,128]{1,0:T(8,128)} %get-tuple-element.15.perturb_ref, f32[128,128]{1,0:T(8,128)} %get-tuple-element.11.out_grad_ref, ...), custom_call_target="tpu_custom_call" | custom-call | tf_op jit(solution)/shard_map/talk2/pallas_call | solution.py:258
  129.9 1.5 fusion.11
  131.4 1.7 fusion.13
  133.1 11.8 %multiply_convert_fusion.1 = (bf16[512,4096]{1,0:T(8,128)(2,1)S(1)}, f32[512,4096]{1,0:T(8,128)}) fusion(bf16[512,1024]{1,0:T(8,128)(2,1)S(1)} %fusion.13, bf16[1024,4096]{1,0:T(8,128)(2,1)} %param.14), kind=kOutput, calls=%fused_computation.7 | convolution fusion | flops 4313841664 | bytes 22020096 | tf_op jit(solution)/shard_map/dot_general | solution.py:309
  145.0 1.9 copy-done
  146.9 2.0 convolution_convert_fusion.partial_ref
  148.9 25.2 %talk3.1 = (bf16[512,1024]{1,0:T(8,128)(2,1)}, f32[128,128]{1,0:T(8,128)}) custom-call(bf16[128,1024]{1,0:T(8,128)(2,1)} %convolution_convert_fusion.partial_ref, bf16[128,128]{1,0:T(8,128)(2,1)} %tokens_ref.5, f32[128,128]{1,0:T(8,128)} %get-tuple-element.34.perturb_ref, f32[128,128]{1,0:T(8,128)} %target_ref.3), custom_call_target="tpu_custom_call" | custom-call | tf_op jit(solution)/shard_map/talk3/pallas_call | solution.py:258
  174.1 19.4 %subtract_convert_fusion.1 = (bf16[256,4096]{1,0:T(8,128)(2,1)}, f32[256,4096]{1,0:T(8,128)}) fusion(bf16[1024,4096]{1,0:T(8,128)(2,1)} %param.14, s32[]{:T(128)S(6)} %select_n.6, f32[256,4096]{1,0:T(8,128)} %fusion.21, f32[512,4096]{1,0:T(8,128)} %get-tuple-element.20, bf16[512,1024]{1,0:T(8,128)(2,1)} %get-tuple-element.14, ...), kind=kOutput, calls=%fused_computation.19 | convolution fusion | flops 5414846464 | bytes 34866176 | tf_op jit(solution)/shard_map/dot_general | solution.py:347
  193.5 9.8 %subtract_convert_fusion = (bf16[4096,256]{1,0:T(8,128)(2,1)}, f32[4096,256]{1,0:T(8,128)}) fusion(bf16[4096,1024]{1,0:T(8,128)(2,1)} %param.15, s32[]{:T(128)S(6)} %select_n.6, f32[4096,256]{1,0:T(8,128)} %fusion.18, bf16[512,4096]{1,0:T(8,128)(2,1)} %copy-done, bf16[512,1024]{1,0:T(8,128)(2,1)} %get-tuple-element.14, f32[4096,256]{1,0:T(8,128)} %param.17), kind=kOutput, calls=%fused_computation.18 | convolution fusion | flops 1082130432 | bytes 21234688 | tf_op jit(solution)/shard_map/dot_general | solution.py:348
  203.3 0.6 copy.16
  (16 shorter events, 0.1 us)
Async XLA Ops:
  38.2 2.0 copy-start.1
  71.3 12.3 %copy-start.2 = (bf16[512,4096]{1,0:T(8,128)(2,1)S(1)}, bf16[512,4096]{1,0:T(8,128)(2,1)}, u32[]{:S(2)}) copy-start(bf16[512,4096]{1,0:T(8,128)(2,1)} %copy-done.1) | copy-start | bytes 12582916
  94.8 36.6 %copy-start.4 = (f32[1024]{0:T(1024)S(1)}, f32[1024]{0:T(1024)}, u32[]{:S(2)}) copy-start(f32[1024]{0:T(1024)} %param.13) | copy-start | bytes 12292
  131.4 15.5 %slice-start = ((s8[8388608]{0:T(1024)(128)(4,1)}), s8[4194304]{0:T(1024)(128)(4,1)S(1)}, s32[]{:S(2)}) async-start(s8[8388608]{0:T(1024)(128)(4,1)} %bitcast.19), calls=%async_computation | async-start | bytes 8388608
  133.1 13.8 %slice-start.1 = ((s8[8388608]{0:T(1024)(128)(4,1)}), s8[4194304]{0:T(1024)(128)(4,1)S(1)}, s32[]{:S(2)}) async-start(s8[8388608]{0:T(1024)(128)(4,1)} %bitcast.19), calls=%async_computation.1 | async-start | bytes 8388608
  145.0 1.9 copy-start
  193.5 9.8 %copy-start.3 = (f32[128,128]{1,0:T(8,128)S(1)}, f32[128,128]{1,0:T(8,128)}, u32[]{:S(2)}) copy-start(f32[128,128]{1,0:T(8,128)} %get-tuple-element.34.perturb_ref) | copy-start | bytes 196612
where the time goes:
time: 204 us
  Pallas kernels  102 us (50%)
  matrix products  86.8 us (43%)
  other arithmetic  7.72 us (4%)
  local copies, waits for them, and re-layouts  6.69 us (3%)
    pallas_call x4, Pallas kernels, talk(): pl.pallas_call(kernel, name=f'talk{number}', out_shape=out_shape, in_spec...  102 us
    dot_general x2, matrix products, shards(): preact = jnp.dot(normed, weight_in, preferred_element_type=jnp.float32)  23.5 us
    dot_general x2, matrix products, shards(): jnp.dot(normed_cols.T, hidden_grad, preferred_element_type=jnp.float32)  22.7 us
    dot_general x2, matrix products, shards(): jnp.dot(hidden.T, grad_cols, preferred_element_type=jnp.float32)  14 us
    dot_general x1, matrix products, shards(): jnp.dot(grad_whole, weight_out.T, preferred_element_type=jnp.float32)  12.3 us
    dot_general x2, matrix products, shards(): jnp.dot(hidden_own, weight_out, preferred_element_type=jnp.float32)  7.37 us
    dot_general x1, matrix products, shards(): jnp.dot(hidden_grad_own, weight_in.T, preferred_element_type=jnp.float32)  6.99 us
    unnamed x15, local copies, waits for them, and re-layouts  4.59 us

commit v1 on v0

v1 whole, which is shorter than its diff:
```python
import functools

import jax
import jax.numpy as jnp
from jax import lax
from jax.experimental import pallas as pl
from jax.experimental.pallas import tpu as pltpu
from jax.sharding import PartitionSpec as P

ASCENTS = 2

coeff = 0.7978845608
cubic = 0.044715
adv_init = 0.5
adv_step = 0.5
decay = 0.9
learn_rate = 0.01
LANES = 128
CHUNK = 256
F32, BF16 = jnp.float32, jnp.bfloat16


def gelu_both(values):
    square = values * values
    half = 0.5 + 0.5 * jnp.tanh(values * (coeff + (coeff * cubic) * square))
    hidden = values * half
    slope = half + (hidden * (1.0 - half)) * (2.0 * coeff + (6.0 * coeff * cubic) * square)
    return hidden, slope


def dot_nt(left, right):
    return lax.dot_general(left, right, (((1,), (1,)), ((), ())), preferred_element_type=F32)


def dot_nn(left, right):
    return jnp.dot(left, right, preferred_element_type=F32)


class Place:
    def __init__(self):
        self.dp_count, self.tensor_count = lax.axis_size("dp"), lax.axis_size("tensor")
        self.ys, self.zs = self.dp_count // 2, self.tensor_count // 2
        self.dp, self.tensor = lax.axis_index("dp"), lax.axis_index("tensor")
        self.y, self.core = self.dp // 2, self.dp % 2
        self.z, self.x = self.tensor // 2, self.tensor % 2


def enter(at):
    barrier = pltpu.get_barrier_semaphore()
    for step in range(1, at.tensor_count):
        there = (at.dp, lax.rem(at.tensor + step, at.tensor_count))
        pl.semaphore_signal(barrier, inc=1, device_id=there, device_id_type=pl.DeviceIdType.MESH)
    for step in range(1, at.dp_count):
        there = (lax.rem(at.dp + step, at.dp_count), at.tensor)
        pl.semaphore_signal(barrier, inc=1, device_id=there, device_id_type=pl.DeviceIdType.MESH)
    pl.semaphore_wait(barrier, at.tensor_count + at.dp_count - 2)


def send(source, target, sems, number, there):
    copy = pltpu.make_async_remote_copy(
        src_ref=source,
        dst_ref=target,
        send_sem=sems[0].at[number],
        recv_sem=sems[1].at[number],
        device_id=there,
        device_id_type=pl.DeviceIdType.MESH,
    )
    copy.start()
    return copy


def gather_copies(dp_count, tensor_count):
    return tensor_count - 1 + dp_count - 1


class Gather:
    def __init__(self, at, own_ref, whole_ref, sems):
        self.at, self.whole, self.sems = at, whole_ref, sems
        self.rows, self.cols = own_ref.shape
        self.numbers = iter(range(gather_copies(at.dp_count, at.tensor_count)))
        self.flat = len(whole_ref.shape) == 2
        self.started = []
        self.other_x = (at.dp, at.z * 2 + 1 - at.x)
        self.partner = (at.y * 2 + 1 - at.core, at.tensor)
        whole_ref[self.place(at.dp, at.tensor)] = own_ref[...]
        self.along_z = [
            self.start(
                own_ref, self.block(at.dp, at.tensor),
                (at.dp, lax.rem(at.z + at.zs - k, at.zs) * 2 + at.x),
            )
            for k in range(1, at.zs)
        ]
        self.along_x = [self.start(own_ref, self.block(at.dp, at.tensor), self.other_x)]

    def span(self, dp):
        return pl.ds(pl.multiple_of(dp * self.rows, self.rows), self.rows)

    def place(self, dp, tensor):
        if self.flat:
            return (self.span(dp), pl.ds(pl.multiple_of(tensor * self.cols, self.cols), self.cols))
        return (tensor, self.span(dp))

    def block(self, dp, tensor):
        return self.whole.at[self.place(dp, tensor)]

    def strip(self, dp):
        return self.whole.at[self.span(dp)] if self.flat else self.whole.at[:, self.span(dp)]

    def start(self, source, target, there):
        copy = send(source, target, self.sems, next(self.numbers), there)
        self.started.append(copy)
        return copy

    def spread(self):
        at = self.at
        for k in range(1, at.zs):
            self.along_z[k - 1].wait_recv()
            block = self.block(at.dp, lax.rem(at.z + k, at.zs) * 2 + at.x)
            self.along_x.append(self.start(block, block, self.other_x))

    def land(self):
        for copy in self.along_x:
            copy.wait_recv()

    def share(self):
        at, strip = self.at, self.strip(self.at.dp)
        self.along_y = {
            j: self.start(
                strip, strip, (lax.rem(at.y + at.ys - j, at.ys) * 2 + at.core, at.tensor)
            )
            for j in range(1, at.ys)
        }
        self.to_core = {0: self.start(strip, strip, self.partner)}

    def from_y(self, j):
        at = self.at
        self.along_y[j].wait_recv()
        strip = self.strip(lax.rem(at.y + j, at.ys) * 2 + at.core)
        self.to_core[j] = self.start(strip, strip, self.partner)

    def from_core(self, j):
        self.to_core[j].wait_recv()

    def done(self):
        for copy in self.started:
            copy.wait_send()

    def row_block(self, dp):
        if self.flat:
            return self.whole[self.span(dp), :]
        return jnp.concatenate(
            [self.whole[t, self.span(dp), :] for t in range(self.at.tensor_count)], axis=1
        )

    def columns_of(self, dp, column, width):
        if self.flat:
            return self.whole[self.span(dp), pl.ds(pl.multiple_of(column, width), width)]
        first = column // self.cols
        return jnp.concatenate(
            [self.whole[first + i, self.span(dp), :] for i in range(width // self.cols)], axis=1
        )


class ScatterSum:
    def __init__(self, at, outgoing, landing, kept, sems):
        self.at, self.outgoing, self.landing, self.kept, self.sems = (
            at, outgoing, landing, kept, sems
        )
        self.cols = outgoing.shape[2]
        self.group = CHUNK // self.cols
        self.chunks = at.tensor_count // self.group
        self.inner = at.tensor % self.group
        self.copies = {}

    def order(self):
        half = self.chunks // 2
        return sorted(range(self.chunks), key=lambda k: (k == 0, abs(k - half)))

    def chunk(self, k):
        return lax.rem(self.at.tensor // self.group + k, self.chunks)

    def give(self, k, value):
        first = self.chunk(k) * self.group
        for i in range(self.group):
            part = value[:, i * self.cols:(i + 1) * self.cols]
            self.outgoing[first + i] = part.astype(BF16)
            if k == 0:
                self.kept[i] = part
        for j in range(self.group):
            label = k * self.group + j
            if label:
                there = first + lax.rem(self.inner + j, self.group)
                self.copies[label] = send(
                    self.outgoing.at[there], self.landing.at[label - 1], self.sems, label - 1,
                    (self.at.dp, there),
                )

    def take(self):
        value = self.kept[self.inner]
        for label, copy in self.copies.items():
            copy.wait_recv()
            value = value + self.landing[label - 1].astype(F32)
        for copy in self.copies.values():
            copy.wait_send()
        return value


class SmallSum:
    def __init__(self, at, axis, out, landing, sems):
        count = at.dp_count if axis == "dp" else at.tensor_count
        self.out, self.landing, self.copies = out, landing, []
        for step in range(1, count):
            if axis == "dp":
                there = (lax.rem(at.dp + step, count), at.tensor)
            else:
                there = (at.dp, lax.rem(at.tensor + step, count))
            self.copies.append(send(out, landing.at[step - 1], sems, step - 1, there))

    def take(self):
        value = self.out[...]
        for step, copy in enumerate(self.copies):
            copy.wait_recv()
            value = value + self.landing[step]
        for copy in self.copies:
            copy.wait_send()
        return value


def own_part(value, offset, size, axis):
    parts = [lax.slice_in_dim(value, s, s + size, axis=axis) for s in range(0, value.shape[axis], size)]
    result = parts[0]
    for i, part in enumerate(parts[1:], 1):
        result = jnp.where(offset == i * size, part, result)
    return result


def step_kernel(
    tokens_ref, noise_ref, ids_ref, target_ref, gain_ref, win_hbm, wout_hbm, min_hbm, mout_hbm,
    hidden, hgrad, turn_in, turn_out, acc_in, acc_out, mom_in, mom_out, own_in, own_out, perturb_ref,
    win, wout, emb_all, grad_all, normed, grad_flat, own_emb, own_grad, out_grad_ref, inv_ref,
    onehot_ref, kept, outgoing, landing_1, landing_2, landing_3,
    table_out, table_in, square_out, square_in, square_out_dp, square_in_dp, count_out, count_in,
    load_sems, late_sems, *sems, scale, features,
):
    at = Place()
    rows, width = tokens_ref.shape
    hidden_units = win.shape[1]
    total = hidden.shape[0]
    own_cols = acc_in.shape[0]
    pairs = [(sems[2 * i], sems[2 * i + 1]) for i in range(len(sems) // 2)]
    gather_sems, sum_sems = pairs[:4], pairs[4:7]
    table_sems, square_sems, square_dp_sems, count_sems = pairs[7:11]
    narrow = len(emb_all.shape) == 3

    loads = [
        pltpu.make_async_copy(win_hbm, win, load_sems.at[0]),
        pltpu.make_async_copy(wout_hbm, wout, load_sems.at[1]),
    ]
    for load in loads:
        load.start()
    block_cols = own_out.shape[1]
    first_col = at.dp * own_cols // block_cols * block_cols
    late = [
        pltpu.make_async_copy(
            win_hbm.at[pl.ds(pl.multiple_of(at.dp * own_cols, own_cols), own_cols)], own_in,
            late_sems.at[0],
        ),
        pltpu.make_async_copy(
            wout_hbm.at[:, pl.ds(pl.multiple_of(first_col, block_cols), block_cols)], own_out,
            late_sems.at[1],
        ),
        pltpu.make_async_copy(min_hbm, mom_in, late_sems.at[2]),
        pltpu.make_async_copy(mout_hbm, mom_out, late_sems.at[3]),
    ]
    tokens = tokens_ref[...].astype(F32)
    own_emb[0] = (tokens + adv_init * noise_ref[...]).astype(BF16)
    enter(at)
    emb = Gather(at, own_emb.at[0], emb_all, gather_sems[0])

    lane = lax.broadcasted_iota(jnp.int32, (rows, rows), 1).astype(F32)
    ids = jnp.broadcast_to(ids_ref[...].astype(F32), (rows, rows)).T
    onehot = (ids == lane).astype(F32)
    onehot_ref[...] = onehot
    count_out[...] = jnp.broadcast_to(jnp.sum(onehot, axis=0, keepdims=True), (8, rows))
    counting = SmallSum(at, "dp", count_out, count_in, count_sems)
    group = max(width, LANES)
    first = at.tensor * width // group * group
    gain_own = own_part(
        gain_ref[:, pl.ds(pl.multiple_of(first, group), group)], at.tensor * width - first, width, 1
    )

    def span(dp):
        return pl.ds(pl.multiple_of(dp * rows, rows), rows)

    def norm(gather, dp, keep=False):
        block = gather.row_block(dp).astype(F32)
        inv = lax.rsqrt(jnp.mean(block * block, axis=1, keepdims=True) + 1e-06)
        normed[span(dp), :] = (block * inv * gain_ref[...]).astype(BF16)
        if keep:
            inv_ref[...] = jnp.broadcast_to(inv, inv_ref.shape)

    tile = 512

    def tiles(body, count=1):
        @pl.loop(0, hidden_units // tile)
        def _(i):
            body(pl.ds(pl.multiple_of(i * tile, tile), tile))

    def forward(dp):
        def body(cols):
            value, slope = gelu_both(dot_nn(normed[span(dp), :], win[:, cols]))
            hidden[span(dp), cols] = value.astype(BF16)
            hgrad[span(dp), cols] = slope.astype(BF16)

        tiles(body)

    def flat_grad(gather, dp):
        if narrow:
            grad_flat[span(dp), :] = gather.row_block(dp)

    grad_source = grad_flat if narrow else grad_all

    def backward(dp):
        def body(cols):
            value = dot_nt(grad_source[span(dp), :], wout[cols, :])
            hgrad[span(dp), cols] = (value * hgrad[span(dp), cols].astype(F32)).astype(BF16)

        tiles(body)

    def turned(source):
        block = max(own_cols, LANES)
        start = at.dp * own_cols // block * block
        value = source[:, pl.ds(pl.multiple_of(start, block), block)].astype(F32).T
        return own_part(value, at.dp * own_cols - start, own_cols, 0).astype(BF16)

    def weight_grads():
        def body(cols):
            acc_in[:, cols] = dot_nn(turn_in[...], hgrad[:, cols])

        tiles(body)

        def body(cols):
            acc_out[:, cols] = dot_nn(turn_out[...], hidden[:, cols])

        tiles(body)

    def partial_out(number, landing):
        sums = ScatterSum(at, outgoing, landing, kept, sum_sems[number])
        for k in sums.order():
            column = pl.multiple_of(sums.chunk(k) * CHUNK, CHUNK)
            sums.give(k, dot_nn(hidden[span(at.dp), :], wout[:, pl.ds(column, CHUNK)]))
        return sums

    def others():
        for j in range(1, at.ys):
            y = lax.rem(at.y + j, at.ys)
            yield j, y * 2 + at.core, y * 2 + 1 - at.core

    partner = at.y * 2 + 1 - at.core

    def finish_forward(sums, perturb, number):
        embedded = tokens_ref[...].astype(F32) + perturb
        out_grad = (embedded + sums.take() - target_ref[...]) * scale
        out_grad_ref[...] = out_grad
        own_grad[number] = out_grad.astype(BF16)

    emb.spread()
    emb.land()
    emb.share()
    norm(emb, at.dp, keep=True)
    loads[0].wait()
    forward(at.dp)
    loads[1].wait()
    sums = partial_out(0, landing_1)
    emb.from_core(0)
    norm(emb, partner)
    forward(partner)
    for j, same, other in others():
        emb.from_y(j)
    finish_forward(sums, adv_init * noise_ref[...], 0)
    grad = Gather(at, own_grad.at[0], grad_all, gather_sems[1])
    for j, same, other in others():
        norm(emb, same)
        forward(same)
    grad.spread()
    grad.land()
    grad.share()
    for load in late:
        load.start()

    flat_grad(grad, at.dp)
    backward(at.dp)
    sums = ScatterSum(at, outgoing, landing_2, kept, sum_sems[1])
    row_dot = jnp.zeros((rows, 1), F32)
    for k in sums.order():
        column = pl.multiple_of(sums.chunk(k) * CHUNK, CHUNK)
        value = dot_nt(hgrad[span(at.dp), :], win[pl.ds(column, CHUNK), :])
        sums.give(k, value)
        along = emb.columns_of(at.dp, column, CHUNK).astype(F32) * gain_ref[:, pl.ds(column, CHUNK)]
        row_dot = row_dot + jnp.sum(value * along, axis=1, keepdims=True)
    table_out[...] = jnp.where(lane == 0.0, row_dot, 0.0).T[:8, :]
    dots = SmallSum(at, "tensor", table_out, table_in, table_sems)
    for j, same, other in others():
        emb.from_core(j)
        norm(emb, other)
        forward(other)
    grad.from_core(0)
    flat_grad(grad, partner)
    for j, same, other in others():
        grad.from_y(j)
    scaled = gain_own * sums.take()
    row_dot = jnp.concatenate([dots.take(), jnp.zeros((rows - 8, rows), F32)], axis=0).T[:, 0:1]
    inv = inv_ref[:, :width]
    radial = own_emb[0].astype(F32) * (inv * inv * inv * (1.0 / features))
    delta = out_grad_ref[...] + inv * scaled - radial * row_dot
    square = jnp.sum(delta * delta, axis=1, keepdims=True)
    square_out[...] = jnp.broadcast_to(
        jnp.sum(onehot_ref[...] * square, axis=0, keepdims=True), (8, rows)
    )
    emb.done()
    squares = SmallSum(at, "tensor", square_out, square_in, square_sems)
    turn_in[...] = turned(normed)
    backward(partner)
    square_out_dp[...] = squares.take()
    squares = SmallSum(at, "dp", square_out_dp, square_in_dp, square_dp_sems)
    for j, same, other in others():
        flat_grad(grad, same)
        backward(same)
    counts = counting.take()
    root_mean = jnp.sqrt(squares.take() / (jnp.maximum(counts, 1.0) * features) + 1e-06)
    token_scale = jnp.sum(onehot_ref[...] * (adv_step / root_mean)[0:1, :], axis=1, keepdims=True)
    perturb = adv_init * noise_ref[...] + delta * token_scale
    perturb_ref[...] = perturb
    own_emb[1] = (tokens_ref[...].astype(F32) + perturb).astype(BF16)

    emb = Gather(at, own_emb.at[1], emb_all, gather_sems[2])
    for j, same, other in others():
        grad.from_core(j)
        flat_grad(grad, other)
        backward(other)
    turn_out[...] = turned(grad_source)
    emb.spread()
    weight_grads()
    grad.done()
    emb.land()
    emb.share()
    norm(emb, at.dp)
    forward(at.dp)
    sums = partial_out(2, landing_3)
    emb.from_core(0)
    norm(emb, partner)
    forward(partner)
    for j, same, other in others():
        emb.from_y(j)
    finish_forward(sums, perturb_ref[...], 1)
    grad = Gather(at, own_grad.at[1], grad_all, gather_sems[3])
    for j, same, other in others():
        norm(emb, same)
        forward(same)
    grad.spread()
    for j, same, other in others():
        emb.from_core(j)
        norm(emb, other)
        forward(other)
    grad.land()
    grad.share()
    turn_in[...] = turned(normed)

    flat_grad(grad, at.dp)
    backward(at.dp)
    grad.from_core(0)
    flat_grad(grad, partner)
    backward(partner)
    for j, same, other in others():
        grad.from_y(j)
        flat_grad(grad, same)
        backward(same)
    for j, same, other in others():
        grad.from_core(j)
        flat_grad(grad, other)
        backward(other)
    turn_out[...] = turned(grad_source)
    emb.done()
    grad.done()
    for load in late:
        load.wait()


def update_kernel(
    hidden, hgrad, turn_in, turn_out, acc_in, acc_out, mom_in, mom_out, own_in, own_out,
    win_hbm, wout_hbm, min_hbm, mout_hbm,
    new_min, new_mout, new_win, new_wout, sems,
):
    at = Place()
    own_cols, hidden_units = acc_in.shape
    block_cols = own_out.shape[1]
    tile = 512
    count = hidden_units // tile

    def copies(i):
        cols = pl.ds(pl.multiple_of(i * tile, tile), tile)
        return [
            pltpu.make_async_copy(new_min.at[:, cols], min_hbm.at[:, cols], sems.at[0, i]),
            pltpu.make_async_copy(new_win.at[:, cols], win_hbm.at[:, cols], sems.at[1, i]),
            pltpu.make_async_copy(new_mout.at[cols], mout_hbm.at[cols], sems.at[2, i]),
            pltpu.make_async_copy(new_wout.at[cols], wout_hbm.at[cols], sems.at[3, i]),
        ]

    offset = at.dp * own_cols - at.dp * own_cols // block_cols * block_cols

    @pl.loop(0, count)
    def _(i):
        cols = pl.ds(pl.multiple_of(i * tile, tile), tile)
        grad = acc_in[:, cols] + dot_nn(turn_in[...], hgrad[:, cols])
        moment = decay * mom_in[:, cols] + grad * (1.0 / ASCENTS)
        new_min[:, cols] = moment
        new_win[:, cols] = (own_in[:, cols].astype(F32) - learn_rate * moment).astype(BF16)
        grad = (acc_out[:, cols] + dot_nn(turn_out[...], hidden[:, cols])).T
        moment = decay * mom_out[cols, :] + grad * (1.0 / ASCENTS)
        new_mout[cols, :] = moment
        own = own_part(own_out[cols, :].astype(F32), offset, own_cols, 1)
        new_wout[cols, :] = (own - learn_rate * moment).astype(BF16)
        for copy in copies(i):
            copy.start()

    @pl.loop(0, count)
    def _(i):
        for copy in copies(i):
            copy.wait()


def room(shapes):
    size = 0
    for shape in shapes:
        if shape.memory_space == pltpu.VMEM:
            *outer, last = shape.shape
            lanes = -(-last // LANES) * LANES
            size += functools.reduce(lambda a, b: a * b, outer, lanes) * jnp.dtype(shape.dtype).itemsize
    return size + 2 * 2**20


def shards(
    tokens, init_noise, segment_ids, target, norm_gain, weight_in, weight_out, moment_in, moment_out
):
    dp_count, tensor_count = lax.axis_size("dp"), lax.axis_size("tensor")
    rows, width = tokens.shape
    features, hidden_units = weight_in.shape
    own_cols = moment_in.shape[0]
    total = rows * dp_count
    narrow = width % LANES != 0
    block_cols = max(own_cols, LANES)
    dma = pltpu.SemaphoreType.DMA
    vmem = pl.BlockSpec(memory_space=pltpu.VMEM)
    anywhere = pl.BlockSpec(memory_space=pl.ANY)
    whole = pltpu.VMEM((tensor_count, total, width) if narrow else (total, features), BF16)
    landing = pltpu.VMEM((tensor_count - 1, rows, width), BF16)
    small = pltpu.VMEM((8, rows), F32)
    over_tensor = pltpu.VMEM((tensor_count - 1, 8, rows), F32)
    over_dp = pltpu.VMEM((dp_count - 1, 8, rows), F32)

    def both(count):
        return [dma((count,)), dma((count,))]

    gather = both(gather_copies(dp_count, tensor_count))
    tensor_sems, dp_sems = both(tensor_count - 1), both(dp_count - 1)
    results = (
        pltpu.VMEM((total, hidden_units), BF16),
        pltpu.VMEM((total, hidden_units), BF16),
        pltpu.VMEM((own_cols, total), BF16),
        pltpu.VMEM((own_cols, total), BF16),
        pltpu.VMEM((own_cols, hidden_units), F32),
        pltpu.VMEM((own_cols, hidden_units), F32),
        pltpu.VMEM((own_cols, hidden_units), F32),
        pltpu.VMEM((hidden_units, own_cols), F32),
        pltpu.VMEM((own_cols, hidden_units), BF16),
        pltpu.VMEM((hidden_units, block_cols), BF16),
    )
    scratch = [
        pltpu.VMEM((features, hidden_units), BF16),
        pltpu.VMEM((hidden_units, features), BF16),
        whole,
        whole,
        pltpu.VMEM((total, features), BF16),
        pltpu.VMEM((total, features) if narrow else (16, LANES), BF16),
        pltpu.VMEM((2, rows, width), BF16),
        pltpu.VMEM((2, rows, width), BF16),
        pltpu.VMEM((rows, width), F32),
        pltpu.VMEM((rows, LANES), F32),
        pltpu.VMEM((rows, rows), F32),
        pltpu.VMEM((CHUNK // width, rows, width), F32),
        pltpu.VMEM((tensor_count, rows, width), BF16),
        landing, landing, landing,
        small, over_tensor, small, over_tensor, small, over_dp, small, over_dp,
        dma((2,)), dma((4,)),
        *gather, *gather, *gather, *gather,
        *tensor_sems, *tensor_sems, *tensor_sems,
        *tensor_sems, *tensor_sems, *dp_sems, *dp_sems,
    ]
    *kept, perturb = pl.pallas_call(
        functools.partial(
            step_kernel, scale=(rows * dp_count) ** (-0.5), features=features
        ),
        name="step",
        out_shape=(*results, jax.ShapeDtypeStruct((rows, width), F32)),
        in_specs=[vmem] * 5 + [anywhere] * 4,
        out_specs=tuple([vmem] * (len(results) + 1)),
        scratch_shapes=scratch,
        compiler_params=pltpu.CompilerParams(
            collective_id=0, has_side_effects=True, vmem_limit_bytes=room(scratch)
        ),
    )(
        tokens, init_noise, segment_ids.reshape(1, rows), target, norm_gain.reshape(1, features),
        weight_in, weight_out, moment_in, moment_out,
    )
    staged = [
        pltpu.VMEM((own_cols, hidden_units), F32),
        pltpu.VMEM((hidden_units, own_cols), F32),
        pltpu.VMEM((own_cols, hidden_units), BF16),
        pltpu.VMEM((hidden_units, own_cols), BF16),
        dma((4, hidden_units // 512)),
    ]
    new_weight_in, new_weight_out, new_moment_in, new_moment_out = pl.pallas_call(
        update_kernel,
        name="update",
        out_shape=(
            jax.ShapeDtypeStruct((own_cols, hidden_units), BF16),
            jax.ShapeDtypeStruct((hidden_units, own_cols), BF16),
            jax.ShapeDtypeStruct((own_cols, hidden_units), F32),
            jax.ShapeDtypeStruct((hidden_units, own_cols), F32),
        ),
        in_specs=[vmem] * len(kept),
        out_specs=(anywhere,) * 4,
        scratch_shapes=staged,
        compiler_params=pltpu.CompilerParams(vmem_limit_bytes=room(staged)),
    )(*kept)
    return (new_weight_in, new_weight_out, new_moment_in, new_moment_out, perturb)


def solution(mesh):
    placed = (
        P("dp", "tensor"),
        P("dp", "tensor"),
        P("dp"),
        P("dp", "tensor"),
        P(),
        P(None, "tensor"),
        P("tensor", None),
        P("dp", "tensor"),
        P("tensor", "dp"),
    )
    return jax.shard_map(
        shards,
        mesh=mesh,
        in_specs=placed,
        out_specs=(
            P("dp", "tensor"),
            P("tensor", "dp"),
            P("dp", "tensor"),
            P("tensor", "dp"),
            P("dp", "tensor"),
        ),
        check_vma=False,
    )
```

time: 204 us -> 110 us (0.54)
  matrix products: 86.8 us -> 0 us
  other arithmetic: 7.72 us -> 0 us
  Pallas kernels: 102 us -> 105 us
  local copies, waits for them, and re-layouts: 6.69 us -> 4.4 us
    dot_general x10 -> x0, matrix products: 86.8 us -> none  [the longest x2 23.5 us: shards(): preact = jnp.dot(normed, weight_in, preferred_element_type=jnp.float32)]
    convert_element_type x2 -> x0, other arithmetic: 3.21 us -> none  [shards(): normed = (gathered * inv_rms * norm_gain).astype(jnp.bfloat16)]
    pallas_call x4 -> x2, Pallas kernels: 102 us -> 105 us  [the longest x1 98.5 us: shards(): pl.pallas_call(functools.partial(step_kernel, scale=(rows * dp_count) **...]
    reduce_sum x2 -> x0, other arithmetic: 3.01 us -> none  [shards(): jnp.mean(gathered * gathered, axis=1, keepdims=True) + 1e-06]
    unnamed x15 -> x11, local copies, waits for them, and re-layouts: 4.59 us -> 4.4 us
where the time goes in v1:
time: 110 us
  Pallas kernels  105 us (95%)
  local copies, waits for them, and re-layouts  4.4 us (4%)
    pallas_call x1, Pallas kernels, shards(): pl.pallas_call(functools.partial(step_kernel, scale=(rows * dp_count) **...  98.5 us
    pallas_call x1, Pallas kernels, shards(): pl.pallas_call(update_kernel, name='update', out_shape=(jax.ShapeDtypeStr...  6.54 us
    unnamed x11, local copies, waits for them, and re-layouts  4.4 us

profile of v1, /device:TPU:0, one launch (start us, length us, event | category | flops | bytes accessed | tf_op | source)
XLA Modules:
  0.0 110.1 jit_solution(6756709548349563547)
XLA Ops:
  0.6 0.0 copy-start
  0.6 0.8 copy-done
  1.5 0.0 copy-start.1
  1.5 0.8 copy-done.1
  2.3 0.0 copy-start.2
  2.3 0.8 copy-done.2
  3.1 0.0 copy-start.3
  3.1 0.7 copy-done.3
  3.8 0.0 copy-start.4
  3.8 0.7 copy-done.4
  4.4 98.5 %step.1 = (bf16[512,4096]{1,0:T(8,128)(2,1)S(1)}, bf16[512,4096]{1,0:T(8,128)(2,1)S(1)}, bf16[256,512]{1,0:T(8,128)(2,1)S(1)}, bf16[256,512]{1,0:T(8,128)(2,1)S(...) custom-call(bf16[128,128]{1,0:T(8,128)(2,1)S(1)} %copy-done.2, ...), custom_call_target="tpu_custom_call" | custom-call | tf_op jit(solution)/shard_map/step/pallas_call | solution.py:599
  102.9 6.5 %update.1 = (bf16[256,4096]{1,0:T(8,128)(2,1)}, bf16[4096,256]{1,0:T(8,128)(2,1)}, f32[256,4096]{1,0:T(8,128)}, f32[4096,256]{1,0:T(8,128)}) custom-call(bf16[512,4096]{1,0:T(8,128)(2,1)S(1)} %get-tuple-element.20.hidden, bf16[512,4096]{1,0:T(8,128)(2,1)S(1)} %get-tuple-element.21.hgrad, bf16[256,512]{1,0:T(8,128)(2,1)S(1)} %get-tuple-element.22.turn_in, ...), custom_call_target="tpu_custom_call" | custom-call | tf_op jit(solution)/shard_map/update/pallas_call | solution.py:622
  109.5 0.6 copy.15
Async XLA Ops:
  0.6 0.8 copy-start
  1.5 0.8 copy-start.1
  2.3 0.8 copy-start.2
  3.1 0.7 copy-start.3
  3.8 0.7 copy-start.4

commit v2 on v1

--- a/solution.py
+++ b/solution.py
@@ -17,6 +17,7 @@
 learn_rate = 0.01
 LANES = 128
 CHUNK = 256
+TILE, TILE_WIDE = 2048, 1024
 F32, BF16 = jnp.float32, jnp.bfloat16
 
 
@@ -70,7 +71,8 @@
 
 
 def gather_copies(dp_count, tensor_count):
-    return tensor_count - 1 + dp_count - 1
+    ys = dp_count // 2
+    return tensor_count - 1 + (ys - 1) * tensor_count + ys
 
 
 class Gather:
@@ -83,14 +85,14 @@
         self.other_x = (at.dp, at.z * 2 + 1 - at.x)
         self.partner = (at.y * 2 + 1 - at.core, at.tensor)
         whole_ref[self.place(at.dp, at.tensor)] = own_ref[...]
+        own = self.block(at.dp, at.tensor)
         self.along_z = [
-            self.start(
-                own_ref, self.block(at.dp, at.tensor),
-                (at.dp, lax.rem(at.z + at.zs - k, at.zs) * 2 + at.x),
-            )
+            self.start(own_ref, own, (at.dp, lax.rem(at.z + at.zs - k, at.zs) * 2 + at.x))
             for k in range(1, at.zs)
         ]
-        self.along_x = [self.start(own_ref, self.block(at.dp, at.tensor), self.other_x)]
+        self.along_x = [self.start(own_ref, own, self.other_x)]
+        self.along_y = {j: [] for j in range(1, at.ys)}
+        self.onward(own_ref, own)
 
     def span(self, dp):
         return pl.ds(pl.multiple_of(dp * self.rows, self.rows), self.rows)
@@ -110,6 +112,12 @@
         copy = send(source, target, self.sems, next(self.numbers), there)
         self.started.append(copy)
         return copy
+
+    def onward(self, source, block):
+        at = self.at
+        for j, copies in self.along_y.items():
+            there = (lax.rem(at.y + at.ys - j, at.ys) * 2 + at.core, at.tensor)
+            copies.append(self.start(source, block, there))
 
     def spread(self):
         at = self.at
@@ -117,24 +125,21 @@
             self.along_z[k - 1].wait_recv()
             block = self.block(at.dp, lax.rem(at.z + k, at.zs) * 2 + at.x)
             self.along_x.append(self.start(block, block, self.other_x))
+            self.onward(block, block)
 
     def land(self):
-        for copy in self.along_x:
+        at = self.at
+        for k, copy in enumerate(self.along_x):
             copy.wait_recv()
-
-    def share(self):
-        at, strip = self.at, self.strip(self.at.dp)
-        self.along_y = {
-            j: self.start(
-                strip, strip, (lax.rem(at.y + at.ys - j, at.ys) * 2 + at.core, at.tensor)
-            )
-            for j in range(1, at.ys)
-        }
+            block = self.block(at.dp, lax.rem(at.z + k, at.zs) * 2 + 1 - at.x)
+            self.onward(block, block)
+        strip = self.strip(at.dp)
         self.to_core = {0: self.start(strip, strip, self.partner)}
 
     def from_y(self, j):
         at = self.at
-        self.along_y[j].wait_recv()
+        for copy in self.along_y[j]:
+            copy.wait_recv()
         strip = self.strip(lax.rem(at.y + j, at.ys) * 2 + at.core)
         self.to_core[j] = self.start(strip, strip, self.partner)
 
@@ -234,10 +239,31 @@
     return result
 
 
+def turned(at, source, own_cols):
+    block = max(own_cols, LANES)
+    start = at.dp * own_cols // block * block
+    value = source[:, pl.ds(pl.multiple_of(start, block), block)].astype(F32).T
+    return own_part(value, at.dp * own_cols - start, own_cols, 0).astype(BF16)
+
+
+def tiles(body, size, tile, part=0, parts=1):
+    share = size // tile // parts
+
+    @pl.loop(part * share, (part + 1) * share)
+    def _(i):
+        body(pl.ds(pl.multiple_of(i * tile, tile), tile))
+
+
+def backward_tile(grad_flat, wout_t, hgrad, span, cols):
+    value = dot_nn(grad_flat[span, :], wout_t[:, cols])
+    hgrad[span, cols] = (value * hgrad[span, cols].astype(F32)).astype(BF16)
+
+
 def step_kernel(
-    tokens_ref, noise_ref, ids_ref, target_ref, gain_ref, win_hbm, wout_hbm, min_hbm, mout_hbm,
-    hidden, hgrad, turn_in, turn_out, acc_in, acc_out, mom_in, mom_out, own_in, own_out, perturb_ref,
-    win, wout, emb_all, grad_all, normed, grad_flat, own_emb, own_grad, out_grad_ref, inv_ref,
+    tokens_hbm, noise_hbm, ids_hbm, target_hbm, gain_hbm, win_hbm, wout_hbm, min_hbm, mout_hbm,
+    hidden, hgrad, turn_in, mom_in, mom_out, own_in, own_out, wout_t, grad_flat, perturb_ref,
+    tokens_ref, noise_ref, ids_ref, target_ref, gain_ref,
+    win, wout, emb_all, grad_3d, normed, own_emb, own_grad, out_grad_ref, inv_ref,
     onehot_ref, kept, outgoing, landing_1, landing_2, landing_3,
     table_out, table_in, square_out, square_in, square_out_dp, square_in_dp, count_out, count_in,
     load_sems, late_sems, *sems, scale, features,
@@ -245,16 +271,18 @@
     at = Place()
     rows, width = tokens_ref.shape
     hidden_units = win.shape[1]
-    total = hidden.shape[0]
-    own_cols = acc_in.shape[0]
+    own_cols = mom_in.shape[0]
     pairs = [(sems[2 * i], sems[2 * i + 1]) for i in range(len(sems) // 2)]
     gather_sems, sum_sems = pairs[:4], pairs[4:7]
     table_sems, square_sems, square_dp_sems, count_sems = pairs[7:11]
     narrow = len(emb_all.shape) == 3
-
+    grad_all = grad_3d if narrow else grad_flat
+
+    small = [(tokens_hbm, tokens_ref), (noise_hbm, noise_ref)]
+    small += [(ids_hbm, ids_ref), (gain_hbm, gain_ref), (target_hbm, target_ref)]
     loads = [
-        pltpu.make_async_copy(win_hbm, win, load_sems.at[0]),
-        pltpu.make_async_copy(wout_hbm, wout, load_sems.at[1]),
+        pltpu.make_async_copy(source, target, load_sems.at[i])
+        for i, (source, target) in enumerate(small + [(wout_hbm, wout), (win_hbm, win)])
     ]
     for load in loads:
         load.start()
@@ -272,8 +300,9 @@
         pltpu.make_async_copy(min_hbm, mom_in, late_sems.at[2]),
         pltpu.make_async_copy(mout_hbm, mom_out, late_sems.at[3]),
     ]
-    tokens = tokens_ref[...].astype(F32)
-    own_emb[0] = (tokens + adv_init * noise_ref[...]).astype(BF16)
+    for load in loads[:5]:
+        load.wait()
+    own_emb[0] = (tokens_ref[...].astype(F32) + adv_init * noise_ref[...]).astype(BF16)
     enter(at)
     emb = Gather(at, own_emb.at[0], emb_all, gather_sems[0])
 
@@ -289,8 +318,8 @@
         gain_ref[:, pl.ds(pl.multiple_of(first, group), group)], at.tensor * width - first, width, 1
     )
 
-    def span(dp):
-        return pl.ds(pl.multiple_of(dp * rows, rows), rows)
+    def span(dp, count=1):
+        return pl.ds(pl.multiple_of(dp * rows, count * rows), count * rows)
 
     def norm(gather, dp, keep=False):
         block = gather.row_block(dp).astype(F32)
@@ -299,50 +328,21 @@
         if keep:
             inv_ref[...] = jnp.broadcast_to(inv, inv_ref.shape)
 
-    tile = 512
-
-    def tiles(body, count=1):
-        @pl.loop(0, hidden_units // tile)
-        def _(i):
-            body(pl.ds(pl.multiple_of(i * tile, tile), tile))
-
-    def forward(dp):
+    def forward(dp, count=1, part=0, parts=1):
         def body(cols):
-            value, slope = gelu_both(dot_nn(normed[span(dp), :], win[:, cols]))
-            hidden[span(dp), cols] = value.astype(BF16)
-            hgrad[span(dp), cols] = slope.astype(BF16)
-
-        tiles(body)
+            value, slope = gelu_both(dot_nn(normed[span(dp, count), :], win[:, cols]))
+            hidden[span(dp, count), cols] = value.astype(BF16)
+            hgrad[span(dp, count), cols] = slope.astype(BF16)
+
+        tiles(body, hidden_units, TILE if count == 1 else TILE_WIDE, part, parts)
 
     def flat_grad(gather, dp):
         if narrow:
             grad_flat[span(dp), :] = gather.row_block(dp)
 
-    grad_source = grad_flat if narrow else grad_all
-
-    def backward(dp):
-        def body(cols):
-            value = dot_nt(grad_source[span(dp), :], wout[cols, :])
-            hgrad[span(dp), cols] = (value * hgrad[span(dp), cols].astype(F32)).astype(BF16)
-
-        tiles(body)
-
-    def turned(source):
-        block = max(own_cols, LANES)
-        start = at.dp * own_cols // block * block
-        value = source[:, pl.ds(pl.multiple_of(start, block), block)].astype(F32).T
-        return own_part(value, at.dp * own_cols - start, own_cols, 0).astype(BF16)
-
-    def weight_grads():
-        def body(cols):
-            acc_in[:, cols] = dot_nn(turn_in[...], hgrad[:, cols])
-
-        tiles(body)
-
-        def body(cols):
-            acc_out[:, cols] = dot_nn(turn_out[...], hidden[:, cols])
-
-        tiles(body)
+    def backward(dp, count=1, part=0, parts=1):
+        body = functools.partial(backward_tile, grad_flat, wout_t, hgrad, span(dp, count))
+        tiles(body, hidden_units, TILE if count == 1 else TILE_WIDE, part, parts)
 
     def partial_out(number, landing):
         sums = ScatterSum(at, outgoing, landing, kept, sum_sems[number])
@@ -351,12 +351,24 @@
             sums.give(k, dot_nn(hidden[span(at.dp), :], wout[:, pl.ds(column, CHUNK)]))
         return sums
 
-    def others():
-        for j in range(1, at.ys):
-            y = lax.rem(at.y + j, at.ys)
-            yield j, y * 2 + at.core, y * 2 + 1 - at.core
-
     partner = at.y * 2 + 1 - at.core
+    planes = [(j, lax.rem(at.y + j, at.ys) * 2) for j in range(1, at.ys)]
+
+    def arrive(gather, then):
+        for j, plane in planes:
+            gather.from_y(j)
+        for j, plane in planes:
+            gather.from_core(j)
+            then(gather, plane)
+            then(gather, plane + 1)
+
+    def forward_planes(part):
+        for j, plane in planes:
+            forward(plane, 2, part, 2)
+
+    def backward_planes(part):
+        for j, plane in planes:
+            backward(plane, 2, part, 2)
 
     def finish_forward(sums, perturb, number):
         embedded = tokens_ref[...].astype(F32) + perturb
@@ -364,29 +376,34 @@
         out_grad_ref[...] = out_grad
         own_grad[number] = out_grad.astype(BF16)
 
+    def turn_weights(part):
+        def body(cols):
+            wout_t[:, cols] = wout[cols, :].T
+
+        tiles(body, hidden_units, 512, part, 2)
+
+    loads[5].wait()
+    turn_weights(0)
     emb.spread()
+    turn_weights(1)
     emb.land()
-    emb.share()
     norm(emb, at.dp, keep=True)
-    loads[0].wait()
+    loads[6].wait()
     forward(at.dp)
-    loads[1].wait()
+    for load in late:
+        load.start()
     sums = partial_out(0, landing_1)
     emb.from_core(0)
     norm(emb, partner)
     forward(partner)
-    for j, same, other in others():
-        emb.from_y(j)
+    arrive(emb, norm)
+    forward_planes(0)
     finish_forward(sums, adv_init * noise_ref[...], 0)
     grad = Gather(at, own_grad.at[0], grad_all, gather_sems[1])
-    for j, same, other in others():
-        norm(emb, same)
-        forward(same)
+    forward_planes(1)
+    turn_in[...] = turned(at, normed, own_cols)
     grad.spread()
     grad.land()
-    grad.share()
-    for load in late:
-        load.start()
 
     flat_grad(grad, at.dp)
     backward(at.dp)
@@ -400,14 +417,11 @@
         row_dot = row_dot + jnp.sum(value * along, axis=1, keepdims=True)
     table_out[...] = jnp.where(lane == 0.0, row_dot, 0.0).T[:8, :]
     dots = SmallSum(at, "tensor", table_out, table_in, table_sems)
-    for j, same, other in others():
-        emb.from_core(j)
-        norm(emb, other)
-        forward(other)
     grad.from_core(0)
     flat_grad(grad, partner)
-    for j, same, other in others():
-        grad.from_y(j)
+    backward(partner)
+    arrive(grad, flat_grad)
+    backward_planes(0)
     scaled = gain_own * sums.take()
     row_dot = jnp.concatenate([dots.take(), jnp.zeros((rows - 8, rows), F32)], axis=0).T[:, 0:1]
     inv = inv_ref[:, :width]
@@ -417,85 +431,76 @@
     square_out[...] = jnp.broadcast_to(
         jnp.sum(onehot_ref[...] * square, axis=0, keepdims=True), (8, rows)
     )
+    out_grad_ref[...] = delta
     emb.done()
     squares = SmallSum(at, "tensor", square_out, square_in, square_sems)
-    turn_in[...] = turned(normed)
-    backward(partner)
+    backward_planes(1)
     square_out_dp[...] = squares.take()
     squares = SmallSum(at, "dp", square_out_dp, square_in_dp, square_dp_sems)
-    for j, same, other in others():
-        flat_grad(grad, same)
-        backward(same)
+    turn_out = turned(at, grad_flat, own_cols)
     counts = counting.take()
     root_mean = jnp.sqrt(squares.take() / (jnp.maximum(counts, 1.0) * features) + 1e-06)
     token_scale = jnp.sum(onehot_ref[...] * (adv_step / root_mean)[0:1, :], axis=1, keepdims=True)
-    perturb = adv_init * noise_ref[...] + delta * token_scale
+    perturb = adv_init * noise_ref[...] + out_grad_ref[...] * token_scale
     perturb_ref[...] = perturb
     own_emb[1] = (tokens_ref[...].astype(F32) + perturb).astype(BF16)
 
     emb = Gather(at, own_emb.at[1], emb_all, gather_sems[2])
-    for j, same, other in others():
-        grad.from_core(j)
-        flat_grad(grad, other)
-        backward(other)
-    turn_out[...] = turned(grad_source)
+    for load in late:
+        load.wait()
+
+    def moment_in_tile(cols):
+        gradient = dot_nn(turn_in[...], hgrad[:, cols])
+        mom_in[:, cols] = decay * mom_in[:, cols] + gradient * (1.0 / ASCENTS)
+
+    def moment_out_tile(cols):
+        gradient = dot_nn(turn_out, hidden[:, cols]).T
+        mom_out[cols, :] = decay * mom_out[cols, :] + gradient * (1.0 / ASCENTS)
+
+    tiles(moment_in_tile, hidden_units, 512)
     emb.spread()
-    weight_grads()
+    tiles(moment_out_tile, hidden_units, 512)
     grad.done()
     emb.land()
-    emb.share()
     norm(emb, at.dp)
     forward(at.dp)
     sums = partial_out(2, landing_3)
     emb.from_core(0)
     norm(emb, partner)
     forward(partner)
-    for j, same, other in others():
-        emb.from_y(j)
+    arrive(emb, norm)
+    forward_planes(0)
     finish_forward(sums, perturb_ref[...], 1)
     grad = Gather(at, own_grad.at[1], grad_all, gather_sems[3])
-    for j, same, other in others():
-        norm(emb, same)
-        forward(same)
+    forward_planes(1)
+    turn_in[...] = turned(at, normed, own_cols)
     grad.spread()
-    for j, same, other in others():
-        emb.from_core(j)
-        norm(emb, other)
-        forward(other)
     grad.land()
-    grad.share()
-    turn_in[...] = turned(normed)
 
     flat_grad(grad, at.dp)
     backward(at.dp)
     grad.from_core(0)
     flat_grad(grad, partner)
     backward(partner)
-    for j, same, other in others():
-        grad.from_y(j)
-        flat_grad(grad, same)
-        backward(same)
-    for j, same, other in others():
-        grad.from_core(j)
-        flat_grad(grad, other)
-        backward(other)
-    turn_out[...] = turned(grad_source)
+    arrive(grad, flat_grad)
     emb.done()
     grad.done()
-    for load in late:
-        load.wait()
 
 
 def update_kernel(
-    hidden, hgrad, turn_in, turn_out, acc_in, acc_out, mom_in, mom_out, own_in, own_out,
-    win_hbm, wout_hbm, min_hbm, mout_hbm,
-    new_min, new_mout, new_win, new_wout, sems,
+    hidden, hgrad, turn_in, mom_in, mom_out, own_in, own_out, wout_t, grad_flat, perturb_ref,
+    win_hbm, wout_hbm, min_hbm, mout_hbm, perturb_hbm,
+    new_min, new_mout, new_win, new_wout, turn_out, perturb_sem, sems,
 ):
     at = Place()
-    own_cols, hidden_units = acc_in.shape
+    own_cols, hidden_units = mom_in.shape
+    pair = perturb_ref.shape[0] * 2
     block_cols = own_out.shape[1]
-    tile = 512
+    tile = 1024
     count = hidden_units // tile
+    perturb_out = pltpu.make_async_copy(perturb_ref, perturb_hbm, perturb_sem)
+    perturb_out.start()
+    turn_out[...] = turned(at, grad_flat, own_cols)
 
     def copies(i):
         cols = pl.ds(pl.multiple_of(i * tile, tile), tile)
@@ -511,15 +516,18 @@
     @pl.loop(0, count)
     def _(i):
         cols = pl.ds(pl.multiple_of(i * tile, tile), tile)
-        grad = acc_in[:, cols] + dot_nn(turn_in[...], hgrad[:, cols])
-        moment = decay * mom_in[:, cols] + grad * (1.0 / ASCENTS)
-        new_min[:, cols] = moment
-        new_win[:, cols] = (own_in[:, cols].astype(F32) - learn_rate * moment).astype(BF16)
-        grad = (acc_out[:, cols] + dot_nn(turn_out[...], hidden[:, cols])).T
-        moment = decay * mom_out[cols, :] + grad * (1.0 / ASCENTS)
+        gradient = dot_nn(turn_out[...], hidden[:, cols]).T
+        moment = decay_rest(mom_out[cols, :], gradient)
         new_mout[cols, :] = moment
         own = own_part(own_out[cols, :].astype(F32), offset, own_cols, 1)
         new_wout[cols, :] = (own - learn_rate * moment).astype(BF16)
+        for j in range(1, at.ys):
+            start = lax.rem(at.y + j, at.ys) * pair
+            backward_tile(grad_flat, wout_t, hgrad, pl.ds(pl.multiple_of(start, pair), pair), cols)
+        gradient = dot_nn(turn_in[...], hgrad[:, cols])
+        moment = decay_rest(mom_in[:, cols], gradient)
+        new_min[:, cols] = moment
+        new_win[:, cols] = (own_in[:, cols].astype(F32) - learn_rate * moment).astype(BF16)
         for copy in copies(i):
             copy.start()
 
@@ -527,6 +535,12 @@
     def _(i):
         for copy in copies(i):
             copy.wait()
+
+    perturb_out.wait()
+
+
+def decay_rest(moment, gradient):
+    return moment + gradient * (1.0 / ASCENTS)
 
 
 def room(shapes):
@@ -536,7 +550,7 @@
             *outer, last = shape.shape
             lanes = -(-last // LANES) * LANES
             size += functools.reduce(lambda a, b: a * b, outer, lanes) * jnp.dtype(shape.dtype).itemsize
-    return size + 2 * 2**20
+    return size + 4 * 2**20
 
 
 def shards(
@@ -551,7 +565,7 @@
     block_cols = max(own_cols, LANES)
     dma = pltpu.SemaphoreType.DMA
     vmem = pl.BlockSpec(memory_space=pltpu.VMEM)
-    anywhere = pl.BlockSpec(memory_space=pl.ANY)
+    anywhere = pl.BlockSpec(memory_space=pltpu.HBM)
     whole = pltpu.VMEM((tensor_count, total, width) if narrow else (total, features), BF16)
     landing = pltpu.VMEM((tensor_count - 1, rows, width), BF16)
     small = pltpu.VMEM((8, rows), F32)
@@ -567,21 +581,25 @@
         pltpu.VMEM((total, hidden_units), BF16),
         pltpu.VMEM((total, hidden_units), BF16),
         pltpu.VMEM((own_cols, total), BF16),
-        pltpu.VMEM((own_cols, total), BF16),
-        pltpu.VMEM((own_cols, hidden_units), F32),
-        pltpu.VMEM((own_cols, hidden_units), F32),
         pltpu.VMEM((own_cols, hidden_units), F32),
         pltpu.VMEM((hidden_units, own_cols), F32),
         pltpu.VMEM((own_cols, hidden_units), BF16),
         pltpu.VMEM((hidden_units, block_cols), BF16),
+        pltpu.VMEM((features, hidden_units), BF16),
+        pltpu.VMEM((total, features), BF16),
+        pltpu.VMEM((rows, width), F32),
     )
     scratch = [
+        pltpu.VMEM((rows, width), BF16),
+        pltpu.VMEM((rows, width), F32),
+        pltpu.VMEM((1, rows), jnp.int32),
+        pltpu.VMEM((rows, width), F32),
+        pltpu.VMEM((1, features), F32),
         pltpu.VMEM((features, hidden_units), BF16),
         pltpu.VMEM((hidden_units, features), BF16),
         whole,
-        whole,
+        whole if narrow else pltpu.VMEM((16, LANES), BF16),
         pltpu.VMEM((total, features), BF16),
-        pltpu.VMEM((total, features) if narrow else (16, LANES), BF16),
         pltpu.VMEM((2, rows, width), BF16),
         pltpu.VMEM((2, rows, width), BF16),
         pltpu.VMEM((rows, width), F32),
@@ -591,35 +609,42 @@
         pltpu.VMEM((tensor_count, rows, width), BF16),
         landing, landing, landing,
         small, over_tensor, small, over_tensor, small, over_dp, small, over_dp,
-        dma((2,)), dma((4,)),
+        dma((7,)), dma((4,)),
         *gather, *gather, *gather, *gather,
         *tensor_sems, *tensor_sems, *tensor_sems,
         *tensor_sems, *tensor_sems, *dp_sems, *dp_sems,
     ]
-    *kept, perturb = pl.pallas_call(
+    kept = pl.pallas_call(
         functools.partial(
             step_kernel, scale=(rows * dp_count) ** (-0.5), features=features
         ),
         name="step",
-        out_shape=(*results, jax.ShapeDtypeStruct((rows, width), F32)),
-        in_specs=[vmem] * 5 + [anywhere] * 4,
-        out_specs=tuple([vmem] * (len(results) + 1)),
+        out_shape=results,
+        in_specs=[anywhere] * 9,
+        out_specs=(vmem,) * len(results),
         scratch_shapes=scratch,
         compiler_params=pltpu.CompilerParams(
             collective_id=0, has_side_effects=True, vmem_limit_bytes=room(scratch)
         ),
     )(
-        tokens, init_noise, segment_ids.reshape(1, rows), target, norm_gain.reshape(1, features),
-        weight_in, weight_out, moment_in, moment_out,
+        *(
+            pltpu.with_memory_space_constraint(array, pltpu.HBM)
+            for array in (
+                tokens, init_noise, segment_ids.reshape(1, rows), target,
+                norm_gain.reshape(1, features), weight_in, weight_out, moment_in, moment_out,
+            )
+        )
     )
     staged = [
         pltpu.VMEM((own_cols, hidden_units), F32),
         pltpu.VMEM((hidden_units, own_cols), F32),
         pltpu.VMEM((own_cols, hidden_units), BF16),
         pltpu.VMEM((hidden_units, own_cols), BF16),
-        dma((4, hidden_units // 512)),
+        pltpu.VMEM((own_cols, total), BF16),
+        dma(()),
+        dma((4, hidden_units // 1024)),
     ]
-    new_weight_in, new_weight_out, new_moment_in, new_moment_out = pl.pallas_call(
+    return pl.pallas_call(
         update_kernel,
         name="update",
         out_shape=(
@@ -627,13 +652,13 @@
             jax.ShapeDtypeStruct((hidden_units, own_cols), BF16),
             jax.ShapeDtypeStruct((own_cols, hidden_units), F32),
             jax.ShapeDtypeStruct((hidden_units, own_cols), F32),
+            jax.ShapeDtypeStruct((rows, width), F32),
         ),
         in_specs=[vmem] * len(kept),
-        out_specs=(anywhere,) * 4,
+        out_specs=(anywhere,) * 5,
         scratch_shapes=staged,
-        compiler_params=pltpu.CompilerParams(vmem_limit_bytes=room(staged)),
+        compiler_params=pltpu.CompilerParams(vmem_limit_bytes=max(room(staged), room(scratch))),
     )(*kept)
-    return (new_weight_in, new_weight_out, new_moment_in, new_moment_out, perturb)
 
 
 def solution(mesh):

time: 110 us -> 94 us (0.85)
  Pallas kernels: 105 us -> 93 us
  local copies, waits for them, and re-layouts: 4.4 us -> 0 us
    pallas_call x1, Pallas kernels: 98.5 us -> 84.6 us  [shards(): pl.pallas_call(functools.partial(step_kernel, scale=(rows * dp_count) **...]
    unnamed x11 -> x0, local copies, waits for them, and re-layouts: 4.4 us -> none
    pallas_call x1, Pallas kernels: 6.54 us -> 8.39 us  [shards(): pl.pallas_call(update_kernel, name='update', out_shape=(jax.ShapeDtypeStr...]
where the time goes in v2:
time: 94 us; the launch traced here: 93.8 us
  Pallas kernels  93 us (99%)
    pallas_call x1, Pallas kernels, shards(): pl.pallas_call(functools.partial(step_kernel, scale=(rows * dp_count) **...  84.6 us
    pallas_call x1, Pallas kernels, shards(): pl.pallas_call(update_kernel, name='update', out_shape=(jax.ShapeDtypeStr...  8.39 us

profile of v2, /device:TPU:0, one launch (start us, length us, event | category | flops | bytes accessed | tf_op | source)
XLA Modules:
  0.0 93.8 jit_solution(7212444095497689124)
XLA Ops:
  0.6 84.6 %step.1 = (bf16[512,4096]{1,0:T(8,128)(2,1)S(1)}, bf16[512,4096]{1,0:T(8,128)(2,1)S(1)}, bf16[256,512]{1,0:T(8,128)(2,1)S(1)}, f32[256,4096]{1,0:T(8,128)S(1)}, ...) custom-call(bf16[128,128]{1,0:T(8,128)(2,1)} %tokens_hbm.1, ...), custom_call_target="tpu_custom_call" | custom-call | tf_op jit(solution)/shard_map/step/pallas_call | solution.py:617
  85.3 8.4 %update.1 = (bf16[256,4096]{1,0:T(8,128)(2,1)}, bf16[4096,256]{1,0:T(8,128)(2,1)}, f32[256,4096]{1,0:T(8,128)}, f32[4096,256]{1,0:T(8,128)}, f32[128,128]{1,0:T(8,128)}) custom-call(bf16[512,4096]{1,0:T(8,128)(2,1)S(1)} %get-tuple-element.15.hidden, bf16[512,4096]{1,0:T(8,128)(2,1)S(1)} %get-tuple-element.16.hgrad, ...), custom_call_target="tpu_custom_call" | custom-call | tf_op jit(solution)/shard_map/update/pallas_call | solution.py:647

commit v3 on v2

--- a/solution.py
+++ b/solution.py
@@ -54,15 +54,18 @@
     for step in range(1, at.dp_count):
         there = (lax.rem(at.dp + step, at.dp_count), at.tensor)
         pl.semaphore_signal(barrier, inc=1, device_id=there, device_id_type=pl.DeviceIdType.MESH)
-    pl.semaphore_wait(barrier, at.tensor_count + at.dp_count - 2)
-
-
-def send(source, target, sems, number, there):
+
+
+def entered(at):
+    pl.semaphore_wait(pltpu.get_barrier_semaphore(), at.tensor_count + at.dp_count - 2)
+
+
+def send(source, target, sems, number, there, landed=None):
     copy = pltpu.make_async_remote_copy(
         src_ref=source,
         dst_ref=target,
         send_sem=sems[0].at[number],
-        recv_sem=sems[1].at[number],
+        recv_sem=sems[1].at[number if landed is None else landed],
         device_id=there,
         device_id_type=pl.DeviceIdType.MESH,
     )
@@ -72,24 +75,35 @@
 
 def gather_copies(dp_count, tensor_count):
     ys = dp_count // 2
-    return tensor_count - 1 + (ys - 1) * tensor_count + ys
+    return tensor_count + (ys - 1) * tensor_count + ys
+
+
+def pack(block):
+    parts = max(1, LANES // block.shape[1])
+    size = block.shape[0] // parts
+    return jnp.concatenate([block[i * size:(i + 1) * size] for i in range(parts)], axis=1)
+
+
+def unpack(block, width):
+    return jnp.concatenate(
+        [block[:, i:i + width] for i in range(0, block.shape[1], width)], axis=0
+    )
 
 
 class Gather:
     def __init__(self, at, own_ref, whole_ref, sems):
         self.at, self.whole, self.sems = at, whole_ref, sems
         self.rows, self.cols = own_ref.shape
-        self.numbers = iter(range(gather_copies(at.dp_count, at.tensor_count)))
+        self.numbers = iter(range(at.zs, gather_copies(at.dp_count, at.tensor_count)))
         self.flat = len(whole_ref.shape) == 2
         self.started = []
         self.other_x = (at.dp, at.z * 2 + 1 - at.x)
         self.partner = (at.y * 2 + 1 - at.core, at.tensor)
         whole_ref[self.place(at.dp, at.tensor)] = own_ref[...]
         own = self.block(at.dp, at.tensor)
-        self.along_z = [
-            self.start(own_ref, own, (at.dp, lax.rem(at.z + at.zs - k, at.zs) * 2 + at.x))
-            for k in range(1, at.zs)
-        ]
+        for m in range(at.zs - 1):
+            there = (at.dp, self.across(m) * 2 + at.x)
+            self.started.append(send(own_ref, own, sems, m, there, landed=at.z))
         self.along_x = [self.start(own_ref, own, self.other_x)]
         self.along_y = {j: [] for j in range(1, at.ys)}
         self.onward(own_ref, own)
@@ -112,6 +126,17 @@
         copy = send(source, target, self.sems, next(self.numbers), there)
         self.started.append(copy)
         return copy
+
+    def across(self, m):
+        at = self.at
+        upper = at.z // (at.zs // 2)
+        last = at.zs - 1 - m
+        down = last - (at.z - last + at.zs) // at.zs
+        up = m + (m - at.z + at.zs) // at.zs
+        return upper * up + (1 - upper) * down
+
+    def nearest(self):
+        return [self.across(m) for m in reversed(range(self.at.zs - 1))]
 
     def onward(self, source, block):
         at = self.at
@@ -121,17 +146,24 @@
 
     def spread(self):
         at = self.at
-        for k in range(1, at.zs):
-            self.along_z[k - 1].wait_recv()
-            block = self.block(at.dp, lax.rem(at.z + k, at.zs) * 2 + at.x)
+        for z in self.nearest():
+            block = self.block(at.dp, z * 2 + at.x)
+            pltpu.make_async_remote_copy(
+                src_ref=block,
+                dst_ref=block,
+                send_sem=self.sems[0].at[0],
+                recv_sem=self.sems[1].at[z],
+                device_id=self.other_x,
+                device_id_type=pl.DeviceIdType.MESH,
+            ).wait_recv()
             self.along_x.append(self.start(block, block, self.other_x))
             self.onward(block, block)
 
     def land(self):
         at = self.at
-        for k, copy in enumerate(self.along_x):
+        for z, copy in zip([at.z] + self.nearest(), self.along_x):
             copy.wait_recv()
-            block = self.block(at.dp, lax.rem(at.z + k, at.zs) * 2 + 1 - at.x)
+            block = self.block(at.dp, z * 2 + 1 - at.x)
             self.onward(block, block)
         strip = self.strip(at.dp)
         self.to_core = {0: self.start(strip, strip, self.partner)}
@@ -150,19 +182,12 @@
         for copy in self.started:
             copy.wait_send()
 
-    def row_block(self, dp):
+    def row_block(self, dp, width):
         if self.flat:
             return self.whole[self.span(dp), :]
         return jnp.concatenate(
-            [self.whole[t, self.span(dp), :] for t in range(self.at.tensor_count)], axis=1
-        )
-
-    def columns_of(self, dp, column, width):
-        if self.flat:
-            return self.whole[self.span(dp), pl.ds(pl.multiple_of(column, width), width)]
-        first = column // self.cols
-        return jnp.concatenate(
-            [self.whole[first + i, self.span(dp), :] for i in range(width // self.cols)], axis=1
+            [unpack(self.whole[t, self.span(dp), :], width) for t in range(self.at.tensor_count)],
+            axis=1,
         )
 
 
@@ -254,6 +279,10 @@
         body(pl.ds(pl.multiple_of(i * tile, tile), tile))
 
 
+def tile_of(at, tile):
+    return tile if at.ys <= 2 else CHUNK
+
+
 def backward_tile(grad_flat, wout_t, hgrad, span, cols):
     value = dot_nn(grad_flat[span, :], wout_t[:, cols])
     hgrad[span, cols] = (value * hgrad[span, cols].astype(F32)).astype(BF16)
@@ -263,8 +292,8 @@
     tokens_hbm, noise_hbm, ids_hbm, target_hbm, gain_hbm, win_hbm, wout_hbm, min_hbm, mout_hbm,
     hidden, hgrad, turn_in, mom_in, mom_out, own_in, own_out, wout_t, grad_flat, perturb_ref,
     tokens_ref, noise_ref, ids_ref, target_ref, gain_ref,
-    win, wout, emb_all, grad_3d, normed, own_emb, own_grad, out_grad_ref, inv_ref,
-    onehot_ref, kept, outgoing, landing_1, landing_2, landing_3,
+    win, wout, emb_all, emb_kept, delta_whole, grad_3d, normed, own_emb, own_grad, out_grad_ref, inv_ref,
+    onehot_ref, scale_ref, kept, outgoing, landing_1, landing_2, landing_3,
     table_out, table_in, square_out, square_in, square_out_dp, square_in_dp, count_out, count_in,
     load_sems, late_sems, *sems, scale, features,
 ):
@@ -277,6 +306,8 @@
     table_sems, square_sems, square_dp_sems, count_sems = pairs[7:11]
     narrow = len(emb_all.shape) == 3
     grad_all = grad_3d if narrow else grad_flat
+    emb_flat = emb_kept if narrow else emb_all
+    delta_all = emb_all if narrow else delta_whole
 
     small = [(tokens_hbm, tokens_ref), (noise_hbm, noise_ref)]
     small += [(ids_hbm, ids_ref), (gain_hbm, gain_ref), (target_hbm, target_ref)]
@@ -300,17 +331,26 @@
         pltpu.make_async_copy(min_hbm, mom_in, late_sems.at[2]),
         pltpu.make_async_copy(mout_hbm, mom_out, late_sems.at[3]),
     ]
+    enter(at)
     for load in loads[:5]:
         load.wait()
-    own_emb[0] = (tokens_ref[...].astype(F32) + adv_init * noise_ref[...]).astype(BF16)
-    enter(at)
+    def first_emb():
+        return (tokens_ref[...].astype(F32) + adv_init * noise_ref[...]).astype(BF16)
+
+    own_emb[0] = pack(first_emb())
+    entered(at)
     emb = Gather(at, own_emb.at[0], emb_all, gather_sems[0])
 
     lane = lax.broadcasted_iota(jnp.int32, (rows, rows), 1).astype(F32)
-    ids = jnp.broadcast_to(ids_ref[...].astype(F32), (rows, rows)).T
-    onehot = (ids == lane).astype(F32)
-    onehot_ref[...] = onehot
-    count_out[...] = jnp.broadcast_to(jnp.sum(onehot, axis=0, keepdims=True), (8, rows))
+
+    def members(ids):
+        return (jnp.broadcast_to(ids, (rows, rows)).T == lane).astype(F32)
+
+    onehot_ref[at.dp] = members(ids_ref[...].astype(F32))
+    count_out[0:4, :] = jnp.broadcast_to(
+        jnp.sum(onehot_ref[at.dp], axis=0, keepdims=True), (4, rows)
+    )
+    count_out[4:8, :] = jnp.broadcast_to(ids_ref[...].astype(F32), (4, rows))
     counting = SmallSum(at, "dp", count_out, count_in, count_sems)
     group = max(width, LANES)
     first = at.tensor * width // group * group
@@ -322,7 +362,17 @@
         return pl.ds(pl.multiple_of(dp * rows, count * rows), count * rows)
 
     def norm(gather, dp, keep=False):
-        block = gather.row_block(dp).astype(F32)
+        block = gather.row_block(dp, width)
+        if narrow:
+            emb_flat[span(dp), :] = block
+        norm_rows(dp, block.astype(F32), keep)
+
+    def norm_moved(gather, dp):
+        step = jnp.sum(onehot_ref[dp] * scale_ref[0:1, :], axis=1, keepdims=True)
+        moved = emb_flat[span(dp), :].astype(F32) + step * gather.row_block(dp, width).astype(F32)
+        norm_rows(dp, moved.astype(BF16).astype(F32), False)
+
+    def norm_rows(dp, block, keep):
         inv = lax.rsqrt(jnp.mean(block * block, axis=1, keepdims=True) + 1e-06)
         normed[span(dp), :] = (block * inv * gain_ref[...]).astype(BF16)
         if keep:
@@ -334,15 +384,15 @@
             hidden[span(dp, count), cols] = value.astype(BF16)
             hgrad[span(dp, count), cols] = slope.astype(BF16)
 
-        tiles(body, hidden_units, TILE if count == 1 else TILE_WIDE, part, parts)
+        tiles(body, hidden_units, tile_of(at, TILE if count == 1 else TILE_WIDE), part, parts)
 
     def flat_grad(gather, dp):
         if narrow:
-            grad_flat[span(dp), :] = gather.row_block(dp)
+            grad_flat[span(dp), :] = gather.row_block(dp, width)
 
     def backward(dp, count=1, part=0, parts=1):
         body = functools.partial(backward_tile, grad_flat, wout_t, hgrad, span(dp, count))
-        tiles(body, hidden_units, TILE if count == 1 else TILE_WIDE, part, parts)
+        tiles(body, hidden_units, tile_of(at, TILE if count == 1 else TILE_WIDE), part, parts)
 
     def partial_out(number, landing):
         sums = ScatterSum(at, outgoing, landing, kept, sum_sems[number])
@@ -374,7 +424,7 @@
         embedded = tokens_ref[...].astype(F32) + perturb
         out_grad = (embedded + sums.take() - target_ref[...]) * scale
         out_grad_ref[...] = out_grad
-        own_grad[number] = out_grad.astype(BF16)
+        own_grad[number] = pack(out_grad.astype(BF16))
 
     def turn_weights(part):
         def body(cols):
@@ -398,11 +448,17 @@
     forward(partner)
     arrive(emb, norm)
     forward_planes(0)
+    emb.done()
     finish_forward(sums, adv_init * noise_ref[...], 0)
     grad = Gather(at, own_grad.at[0], grad_all, gather_sems[1])
     forward_planes(1)
+    grad.spread()
     turn_in[...] = turned(at, normed, own_cols)
-    grad.spread()
+    counts = counting.take()
+    scale_ref[...] = jnp.maximum(counts, 1.0) * features
+    for step in range(1, at.dp_count):
+        ids = count_in[step - 1, 4:5, :]
+        onehot_ref[lax.rem(at.dp + at.dp_count - step, at.dp_count)] = members(ids)
     grad.land()
 
     flat_grad(grad, at.dp)
@@ -413,7 +469,7 @@
         column = pl.multiple_of(sums.chunk(k) * CHUNK, CHUNK)
         value = dot_nt(hgrad[span(at.dp), :], win[pl.ds(column, CHUNK), :])
         sums.give(k, value)
-        along = emb.columns_of(at.dp, column, CHUNK).astype(F32) * gain_ref[:, pl.ds(column, CHUNK)]
+        along = emb_flat[span(at.dp), pl.ds(column, CHUNK)].astype(F32) * gain_ref[:, pl.ds(column, CHUNK)]
         row_dot = row_dot + jnp.sum(value * along, axis=1, keepdims=True)
     table_out[...] = jnp.where(lane == 0.0, row_dot, 0.0).T[:8, :]
     dots = SmallSum(at, "tensor", table_out, table_in, table_sems)
@@ -425,27 +481,21 @@
     scaled = gain_own * sums.take()
     row_dot = jnp.concatenate([dots.take(), jnp.zeros((rows - 8, rows), F32)], axis=0).T[:, 0:1]
     inv = inv_ref[:, :width]
-    radial = own_emb[0].astype(F32) * (inv * inv * inv * (1.0 / features))
+    radial = first_emb().astype(F32) * (inv * inv * inv * (1.0 / features))
     delta = out_grad_ref[...] + inv * scaled - radial * row_dot
     square = jnp.sum(delta * delta, axis=1, keepdims=True)
     square_out[...] = jnp.broadcast_to(
-        jnp.sum(onehot_ref[...] * square, axis=0, keepdims=True), (8, rows)
-    )
+        jnp.sum(onehot_ref[at.dp] * square, axis=0, keepdims=True), (8, rows)
+    )
+    squares = SmallSum(at, "tensor", square_out, square_in, square_sems)
     out_grad_ref[...] = delta
-    emb.done()
-    squares = SmallSum(at, "tensor", square_out, square_in, square_sems)
+    own_emb[1] = pack(delta.astype(BF16))
+    emb = Gather(at, own_emb.at[1], delta_all, gather_sems[2])
     backward_planes(1)
+    emb.spread()
     square_out_dp[...] = squares.take()
     squares = SmallSum(at, "dp", square_out_dp, square_in_dp, square_dp_sems)
     turn_out = turned(at, grad_flat, own_cols)
-    counts = counting.take()
-    root_mean = jnp.sqrt(squares.take() / (jnp.maximum(counts, 1.0) * features) + 1e-06)
-    token_scale = jnp.sum(onehot_ref[...] * (adv_step / root_mean)[0:1, :], axis=1, keepdims=True)
-    perturb = adv_init * noise_ref[...] + out_grad_ref[...] * token_scale
-    perturb_ref[...] = perturb
-    own_emb[1] = (tokens_ref[...].astype(F32) + perturb).astype(BF16)
-
-    emb = Gather(at, own_emb.at[1], emb_all, gather_sems[2])
     for load in late:
         load.wait()
 
@@ -458,17 +508,21 @@
         mom_out[cols, :] = decay * mom_out[cols, :] + gradient * (1.0 / ASCENTS)
 
     tiles(moment_in_tile, hidden_units, 512)
-    emb.spread()
-    tiles(moment_out_tile, hidden_units, 512)
     grad.done()
     emb.land()
-    norm(emb, at.dp)
+    tiles(moment_out_tile, hidden_units, 512)
+    root_mean = jnp.sqrt(squares.take() / scale_ref[...] + 1e-06)
+    scale_ref[...] = adv_step / root_mean
+    token_scale = jnp.sum(onehot_ref[at.dp] * scale_ref[0:1, :], axis=1, keepdims=True)
+    perturb_ref[...] = adv_init * noise_ref[...] + out_grad_ref[...] * token_scale
+
+    norm_moved(emb, at.dp)
     forward(at.dp)
     sums = partial_out(2, landing_3)
     emb.from_core(0)
-    norm(emb, partner)
+    norm_moved(emb, partner)
     forward(partner)
-    arrive(emb, norm)
+    arrive(emb, norm_moved)
     forward_planes(0)
     finish_forward(sums, perturb_ref[...], 1)
     grad = Gather(at, own_grad.at[1], grad_all, gather_sems[3])
@@ -496,7 +550,7 @@
     own_cols, hidden_units = mom_in.shape
     pair = perturb_ref.shape[0] * 2
     block_cols = own_out.shape[1]
-    tile = 1024
+    tile = tile_of(at, 1024)
     count = hidden_units // tile
     perturb_out = pltpu.make_async_copy(perturb_ref, perturb_hbm, perturb_sem)
     perturb_out.start()
@@ -550,7 +604,7 @@
             *outer, last = shape.shape
             lanes = -(-last // LANES) * LANES
             size += functools.reduce(lambda a, b: a * b, outer, lanes) * jnp.dtype(shape.dtype).itemsize
-    return size + 4 * 2**20
+    return size + int(3.25 * 2**20)
 
 
 def shards(
@@ -566,9 +620,13 @@
     dma = pltpu.SemaphoreType.DMA
     vmem = pl.BlockSpec(memory_space=pltpu.VMEM)
     anywhere = pl.BlockSpec(memory_space=pltpu.HBM)
-    whole = pltpu.VMEM((tensor_count, total, width) if narrow else (total, features), BF16)
+    parts = max(1, LANES // width)
+    whole = pltpu.VMEM(
+        (tensor_count, total // parts, width * parts) if narrow else (total, features), BF16
+    )
     landing = pltpu.VMEM((tensor_count - 1, rows, width), BF16)
     small = pltpu.VMEM((8, rows), F32)
+    unused = pltpu.VMEM((16, LANES), BF16)
     over_tensor = pltpu.VMEM((tensor_count - 1, 8, rows), F32)
     over_dp = pltpu.VMEM((dp_count - 1, 8, rows), F32)
 
@@ -598,13 +656,16 @@
         pltpu.VMEM((features, hidden_units), BF16),
         pltpu.VMEM((hidden_units, features), BF16),
         whole,
-        whole if narrow else pltpu.VMEM((16, LANES), BF16),
+        pltpu.VMEM((total, features), BF16) if narrow else unused,
+        unused if narrow else whole,
+        whole if narrow else unused,
         pltpu.VMEM((total, features), BF16),
-        pltpu.VMEM((2, rows, width), BF16),
-        pltpu.VMEM((2, rows, width), BF16),
+        pltpu.VMEM((2, rows // parts, width * parts), BF16),
+        pltpu.VMEM((2, rows // parts, width * parts), BF16),
         pltpu.VMEM((rows, width), F32),
         pltpu.VMEM((rows, LANES), F32),
-        pltpu.VMEM((rows, rows), F32),
+        pltpu.VMEM((dp_count, rows, rows), F32),
+        small,
         pltpu.VMEM((CHUNK // width, rows, width), F32),
         pltpu.VMEM((tensor_count, rows, width), BF16),
         landing, landing, landing,
@@ -642,7 +703,7 @@
         pltpu.VMEM((hidden_units, own_cols), BF16),
         pltpu.VMEM((own_cols, total), BF16),
         dma(()),
-        dma((4, hidden_units // 1024)),
+        dma((4, hidden_units // CHUNK)),
     ]
     return pl.pallas_call(
         update_kernel,

time: 94 us -> 92.1 us (0.980)
  Pallas kernels: 93 us -> 91.1 us
    pallas_call x1, Pallas kernels: 84.6 us -> 82.2 us  [shards(): pl.pallas_call(functools.partial(step_kernel, scale=(rows * dp_count) **...]
where the time goes in v3:
time: 92.1 us; the launch traced here: 91.9 us
  Pallas kernels  91.1 us (99%)
    pallas_call x1, Pallas kernels, shards(): pl.pallas_call(functools.partial(step_kernel, scale=(rows * dp_count) **...  82.2 us
    pallas_call x1, Pallas kernels, shards(): pl.pallas_call(update_kernel, name='update', out_shape=(jax.ShapeDtypeStr...  8.86 us

profile of v3, /device:TPU:0, one launch (start us, length us, event | category | flops | bytes accessed | tf_op | source)
XLA Modules:
  0.0 91.9 jit_solution(11517418428584136373)
XLA Ops:
  0.6 82.2 %step.1 = (bf16[512,4096]{1,0:T(8,128)(2,1)S(1)}, bf16[512,4096]{1,0:T(8,128)(2,1)S(1)}, bf16[256,512]{1,0:T(8,128)(2,1)S(1)}, f32[256,4096]{1,0:T(8,128)S(1)}, ...) custom-call(bf16[128,128]{1,0:T(8,128)(2,1)} %tokens_hbm.1, ...), custom_call_target="tpu_custom_call" | custom-call | tf_op jit(solution)/shard_map/step/pallas_call | solution.py:678
  82.9 8.9 %update.1 = (bf16[256,4096]{1,0:T(8,128)(2,1)}, bf16[4096,256]{1,0:T(8,128)(2,1)}, f32[256,4096]{1,0:T(8,128)}, f32[4096,256]{1,0:T(8,128)}, f32[128,128]{1,0:T(8,128)}) custom-call(bf16[512,4096]{1,0:T(8,128)(2,1)S(1)} %get-tuple-element.15.hidden, bf16[512,4096]{1,0:T(8,128)(2,1)S(1)} %get-tuple-element.16.hgrad, ...), custom_call_target="tpu_custom_call" | custom-call | tf_op jit(solution)/shard_map/update/pallas_call | solution.py:708

commit v4 on v3

--- a/solution.py
+++ b/solution.py
@@ -344,11 +344,11 @@
     lane = lax.broadcasted_iota(jnp.int32, (rows, rows), 1).astype(F32)
 
     def members(ids):
-        return (jnp.broadcast_to(ids, (rows, rows)).T == lane).astype(F32)
+        return (jnp.broadcast_to(ids, (rows, rows)).T == lane).astype(BF16)
 
     onehot_ref[at.dp] = members(ids_ref[...].astype(F32))
     count_out[0:4, :] = jnp.broadcast_to(
-        jnp.sum(onehot_ref[at.dp], axis=0, keepdims=True), (4, rows)
+        jnp.sum(onehot_ref[at.dp].astype(F32), axis=0, keepdims=True), (4, rows)
     )
     count_out[4:8, :] = jnp.broadcast_to(ids_ref[...].astype(F32), (4, rows))
     counting = SmallSum(at, "dp", count_out, count_in, count_sems)
@@ -368,7 +368,7 @@
         norm_rows(dp, block.astype(F32), keep)
 
     def norm_moved(gather, dp):
-        step = jnp.sum(onehot_ref[dp] * scale_ref[0:1, :], axis=1, keepdims=True)
+        step = jnp.sum(onehot_ref[dp].astype(F32) * scale_ref[0:1, :], axis=1, keepdims=True)
         moved = emb_flat[span(dp), :].astype(F32) + step * gather.row_block(dp, width).astype(F32)
         norm_rows(dp, moved.astype(BF16).astype(F32), False)
 
@@ -414,7 +414,7 @@
 
     def forward_planes(part):
         for j, plane in planes:
-            forward(plane, 2, part, 2)
+            forward(plane, 2, part, 4)
 
     def backward_planes(part):
         for j, plane in planes:
@@ -424,7 +424,7 @@
         embedded = tokens_ref[...].astype(F32) + perturb
         out_grad = (embedded + sums.take() - target_ref[...]) * scale
         out_grad_ref[...] = out_grad
-        own_grad[number] = pack(out_grad.astype(BF16))
+        own_grad[0] = pack(out_grad.astype(BF16))
 
     def turn_weights(part):
         def body(cols):
@@ -432,10 +432,9 @@
 
         tiles(body, hidden_units, 512, part, 2)
 
+    emb.spread()
     loads[5].wait()
     turn_weights(0)
-    emb.spread()
-    turn_weights(1)
     emb.land()
     norm(emb, at.dp, keep=True)
     loads[6].wait()
@@ -453,6 +452,9 @@
     grad = Gather(at, own_grad.at[0], grad_all, gather_sems[1])
     forward_planes(1)
     grad.spread()
+    forward_planes(2)
+    forward_planes(3)
+    turn_weights(1)
     turn_in[...] = turned(at, normed, own_cols)
     counts = counting.take()
     scale_ref[...] = jnp.maximum(counts, 1.0) * features
@@ -485,12 +487,12 @@
     delta = out_grad_ref[...] + inv * scaled - radial * row_dot
     square = jnp.sum(delta * delta, axis=1, keepdims=True)
     square_out[...] = jnp.broadcast_to(
-        jnp.sum(onehot_ref[at.dp] * square, axis=0, keepdims=True), (8, rows)
+        jnp.sum(onehot_ref[at.dp].astype(F32) * square, axis=0, keepdims=True), (8, rows)
     )
     squares = SmallSum(at, "tensor", square_out, square_in, square_sems)
     out_grad_ref[...] = delta
-    own_emb[1] = pack(delta.astype(BF16))
-    emb = Gather(at, own_emb.at[1], delta_all, gather_sems[2])
+    own_emb[0] = pack(delta.astype(BF16))
+    emb = Gather(at, own_emb.at[0], delta_all, gather_sems[2])
     backward_planes(1)
     emb.spread()
     square_out_dp[...] = squares.take()
@@ -507,13 +509,13 @@
         gradient = dot_nn(turn_out, hidden[:, cols]).T
         mom_out[cols, :] = decay * mom_out[cols, :] + gradient * (1.0 / ASCENTS)
 
-    tiles(moment_in_tile, hidden_units, 512)
+    tiles(moment_in_tile, hidden_units, tile_of(at, 1024))
     grad.done()
     emb.land()
-    tiles(moment_out_tile, hidden_units, 512)
+    tiles(moment_out_tile, hidden_units, tile_of(at, 1024))
     root_mean = jnp.sqrt(squares.take() / scale_ref[...] + 1e-06)
     scale_ref[...] = adv_step / root_mean
-    token_scale = jnp.sum(onehot_ref[at.dp] * scale_ref[0:1, :], axis=1, keepdims=True)
+    token_scale = jnp.sum(onehot_ref[at.dp].astype(F32) * scale_ref[0:1, :], axis=1, keepdims=True)
     perturb_ref[...] = adv_init * noise_ref[...] + out_grad_ref[...] * token_scale
 
     norm_moved(emb, at.dp)
@@ -525,10 +527,12 @@
     arrive(emb, norm_moved)
     forward_planes(0)
     finish_forward(sums, perturb_ref[...], 1)
-    grad = Gather(at, own_grad.at[1], grad_all, gather_sems[3])
+    grad = Gather(at, own_grad.at[0], grad_all, gather_sems[3])
     forward_planes(1)
+    grad.spread()
+    forward_planes(2)
+    forward_planes(3)
     turn_in[...] = turned(at, normed, own_cols)
-    grad.spread()
     grad.land()
 
     flat_grad(grad, at.dp)
@@ -604,7 +608,7 @@
             *outer, last = shape.shape
             lanes = -(-last // LANES) * LANES
             size += functools.reduce(lambda a, b: a * b, outer, lanes) * jnp.dtype(shape.dtype).itemsize
-    return size + int(3.25 * 2**20)
+    return size + int(3.9 * 2**20)
 
 
 def shards(
@@ -660,11 +664,11 @@
         unused if narrow else whole,
         whole if narrow else unused,
         pltpu.VMEM((total, features), BF16),
-        pltpu.VMEM((2, rows // parts, width * parts), BF16),
-        pltpu.VMEM((2, rows // parts, width * parts), BF16),
+        pltpu.VMEM((1, rows // parts, width * parts), BF16),
+        pltpu.VMEM((1, rows // parts, width * parts), BF16),
         pltpu.VMEM((rows, width), F32),
         pltpu.VMEM((rows, LANES), F32),
-        pltpu.VMEM((dp_count, rows, rows), F32),
+        pltpu.VMEM((dp_count, rows, rows), BF16),
         small,
         pltpu.VMEM((CHUNK // width, rows, width), F32),
         pltpu.VMEM((tensor_count, rows, width), BF16),

time: 92.1 us -> 89.1 us (0.967)
  Pallas kernels: 91.1 us -> 88.1 us
    pallas_call x1, Pallas kernels: 82.2 us -> 79.3 us  [shards(): pl.pallas_call(functools.partial(step_kernel, scale=(rows * dp_count) **...]
where the time goes in v4:
time: 89.1 us; the launch traced here: 88.9 us
  Pallas kernels  88.1 us (99%)
    pallas_call x1, Pallas kernels, shards(): pl.pallas_call(functools.partial(step_kernel, scale=(rows * dp_count) **...  79.3 us
    pallas_call x1, Pallas kernels, shards(): pl.pallas_call(update_kernel, name='update', out_shape=(jax.ShapeDtypeStr...  8.84 us

profile of v4, /device:TPU:0, one launch (start us, length us, event | category | flops | bytes accessed | tf_op | source)
XLA Modules:
  0.0 88.9 jit_solution(2953412501977623563)
XLA Ops:
  0.6 79.3 %step.1 = (bf16[512,4096]{1,0:T(8,128)(2,1)S(1)}, bf16[512,4096]{1,0:T(8,128)(2,1)S(1)}, bf16[256,512]{1,0:T(8,128)(2,1)S(1)}, f32[256,4096]{1,0:T(8,128)S(1)}, ...) custom-call(bf16[128,128]{1,0:T(8,128)(2,1)} %tokens_hbm.1, ...), custom_call_target="tpu_custom_call" | custom-call | tf_op jit(solution)/shard_map/step/pallas_call | solution.py:682
  79.9 8.8 %update.1 = (bf16[256,4096]{1,0:T(8,128)(2,1)}, bf16[4096,256]{1,0:T(8,128)(2,1)}, f32[256,4096]{1,0:T(8,128)}, f32[4096,256]{1,0:T(8,128)}, f32[128,128]{1,0:T(8,128)}) custom-call(bf16[512,4096]{1,0:T(8,128)(2,1)S(1)} %get-tuple-element.15.hidden, bf16[512,4096]{1,0:T(8,128)(2,1)S(1)} %get-tuple-element.16.hgrad, ...), custom_call_target="tpu_custom_call" | custom-call | tf_op jit(solution)/shard_map/update/pallas_call | solution.py:712

commit v5 on v4

--- a/solution.py
+++ b/solution.py
@@ -446,12 +446,12 @@
     norm(emb, partner)
     forward(partner)
     arrive(emb, norm)
-    forward_planes(0)
     emb.done()
     finish_forward(sums, adv_init * noise_ref[...], 0)
     grad = Gather(at, own_grad.at[0], grad_all, gather_sems[1])
     forward_planes(1)
     grad.spread()
+    forward_planes(0)
     forward_planes(2)
     forward_planes(3)
     turn_weights(1)
@@ -525,11 +525,11 @@
     norm_moved(emb, partner)
     forward(partner)
     arrive(emb, norm_moved)
-    forward_planes(0)
     finish_forward(sums, perturb_ref[...], 1)
     grad = Gather(at, own_grad.at[0], grad_all, gather_sems[3])
     forward_planes(1)
     grad.spread()
+    forward_planes(0)
     forward_planes(2)
     forward_planes(3)
     turn_in[...] = turned(at, normed, own_cols)

time: 89.1 us -> 90.6 us (1.017)
  Pallas kernels: 88.1 us -> 89.6 us
    pallas_call x1, Pallas kernels: 79.3 us -> 80.8 us  [shards(): pl.pallas_call(functools.partial(step_kernel, scale=(rows * dp_count) **...]
where the time goes in v5:
time: 90.6 us; the launch traced here: 90.4 us
  Pallas kernels  89.6 us (99%)
    pallas_call x1, Pallas kernels, shards(): pl.pallas_call(functools.partial(step_kernel, scale=(rows * dp_count) **...  80.8 us
    pallas_call x1, Pallas kernels, shards(): pl.pallas_call(update_kernel, name='update', out_shape=(jax.ShapeDtypeStr...  8.82 us

profile of v5, /device:TPU:0, one launch (start us, length us, event | category | flops | bytes accessed | tf_op | source)
XLA Modules:
  0.0 90.4 jit_solution(15655088562675303192)
XLA Ops:
  0.6 80.8 %step.1 = (bf16[512,4096]{1,0:T(8,128)(2,1)S(1)}, bf16[512,4096]{1,0:T(8,128)(2,1)S(1)}, bf16[256,512]{1,0:T(8,128)(2,1)S(1)}, f32[256,4096]{1,0:T(8,128)S(1)}, ...) custom-call(bf16[128,128]{1,0:T(8,128)(2,1)} %tokens_hbm.1, ...), custom_call_target="tpu_custom_call" | custom-call | tf_op jit(solution)/shard_map/step/pallas_call | solution.py:682
  81.4 8.8 %update.1 = (bf16[256,4096]{1,0:T(8,128)(2,1)}, bf16[4096,256]{1,0:T(8,128)(2,1)}, f32[256,4096]{1,0:T(8,128)}, f32[4096,256]{1,0:T(8,128)}, f32[128,128]{1,0:T(8,128)}) custom-call(bf16[512,4096]{1,0:T(8,128)(2,1)S(1)} %get-tuple-element.15.hidden, bf16[512,4096]{1,0:T(8,128)(2,1)S(1)} %get-tuple-element.16.hgrad, ...), custom_call_target="tpu_custom_call" | custom-call | tf_op jit(solution)/shard_map/update/pallas_call | solution.py:712
